TPU v7x, 512 devices: a 8x2x16 block of a 8x8x16 slice. The times are simulated.
512 devices in a mesh: grp: 2 (over y), shot: 16 (over x, core), slab: 16 (over z).
Axes of the slice: x: 8, y: 2, z: 16, core: 2. Of those that a mesh axis runs over, the one named last changes fastest.
The devices are a block of a 8x8x16 slice.
Arguments:
- courant_sq: float32 [2048, 1024], P(('grp', 'slab')), parts along dimension 0, may hold values from 0.05 to 0.25
- sponge_level: int32 [2048, 1024], P(('grp', 'slab')), parts along dimension 0, may hold values from 0 to 3
- source_later: float32 [64, 1024, 1024], P(('grp', 'shot'), 'slab'), parts along dimension 0, may hold values from -6 to 6
- source_now: float32 [64, 1024, 1024], P(('grp', 'shot'), 'slab'), parts along dimension 0, may hold values from -6 to 6
- receiver_later: float32 [64, 1024, 1024], P(('grp', 'shot'), 'slab'), parts along dimension 0, may hold values from -6 to 6
- receiver_now: float32 [64, 1024, 1024], P(('grp', 'shot'), 'slab'), parts along dimension 0, may hold values from -6 to 6
- traces: float32 [64, 16, 512], P(('grp', 'shot')), parts along dimension 0, may hold values from -24 to 24
- wavelet: float32 [512], P('grp'), parts along dimension 0, may hold values from -24 to 24
- source_depth: int32 [64], P(('grp', 'shot')), parts along dimension 0, may hold values from 0 to 1023
- source_lateral: int32 [64], P(('grp', 'shot')), parts along dimension 0, may hold values from 0 to 1023
- receiver_depth: int32 [64, 512], P(('grp', 'shot')), parts along dimension 0, may hold values from 0 to 1023
- receiver_lateral: int32 [64, 512], P(('grp', 'shot')), parts along dimension 0, may hold values from 0 to 1023
- checkpoint_step: int32 [64], P(('grp', 'shot')), parts along dimension 0, may hold values from 0 to 240
Outputs:
- image: float32 [2048, 1024], P(('grp', 'slab')), parts along dimension 0
- source_out: float32 [64, 1024, 1024], P(('grp', 'shot'), 'slab'), parts along dimension 0
- receiver_out: float32 [64, 1024, 1024], P(('grp', 'shot'), 'slab'), parts along dimension 0
There are 2 independent parts, one for each index of `grp`. A program takes and returns all parts, laid end to end along the dimension named above; each array names one. Nothing has to cross between parts.
All inputs are finite; a program needn't handle non-finite values.
Results may differ from a plain program's by a relative error of at most 0.0003.
Values sent between devices are 32-bit elements; how exact they have to be, the bound alone decides.
A program may use at most 64 MiB of HBM per device.

v0:
```python
import math

import jax
import jax.numpy as jnp
from jax import lax
from jax.sharding import PartitionSpec as P

STEPS = 16


stencil_coeffs = (-205.0 / 72.0, 8.0 / 5.0, -1.0 / 5.0, 8.0 / 315.0, -1.0 / 560.0)


def extended_2(cells, sides, width):
    for axis, dim in sides:
        count = lax.axis_size(axis)
        ends = count - 1
        head = lax.slice_in_dim(cells, 0, width, axis=dim)
        tail = lax.slice_in_dim(cells, cells.shape[dim] - width, cells.shape[dim], axis=dim)
        cells = jnp.concatenate(
            [
                lax.ppermute(tail, axis, [(i, (i + 1) % count) for i in range(ends)]),
                cells,
                lax.ppermute(head, axis, [((i + 1) % count, i) for i in range(ends)]),
            ],
            axis=dim,
        )
    return cells


def gathered_total(shard, axis):
    blocks = lax.all_gather(shard, axis)
    return blocks.sum(axis=0)


def laplace(extended):
    row_count = extended.shape[-2] - 8
    width = extended.shape[-1]
    centre = extended[..., 4 : 4 + row_count, :]
    pad_spec = [(0, 0)] * (centre.ndim - 1) + [(4, 4)]
    padded = jnp.pad(centre, pad_spec)
    result = 2.0 * stencil_coeffs[0] * centre
    for offset in range(1, 5):
        result = result + stencil_coeffs[offset] * (
            extended[..., 4 + offset : 4 + offset + row_count, :]
            + extended[..., 4 - offset : 4 - offset + row_count, :]
            + padded[..., 4 + offset : 4 + offset + width]
            + padded[..., 4 - offset : 4 - offset + width]
        )
    return result


def local(
    courant_sq,
    sponge_level,
    source_later,
    source_now,
    receiver_later,
    receiver_now,
    traces,
    wavelet,
    source_depth,
    source_lateral,
    receiver_depth,
    receiver_lateral,
    checkpoint_step,
):
    slab_rows = courant_sq.shape[0]
    lateral_cells = courant_sq.shape[1]
    first_row = lax.axis_index("slab") * slab_rows
    damping = 1.0 - 0.06 * sponge_level.astype(jnp.float32)
    lateral_ids = jnp.arange(lateral_cells, dtype=jnp.int32)
    lateral_table = (receiver_lateral[:, :, None] == lateral_ids[None, None, :]).astype(jnp.float32)
    source_column = lateral_ids[None, :] == source_lateral[:, None]

    def advance(src_now, src_hi, rec_now, rec_hi, laplacian, velocity, damper, top_row, step_index):
        row_count = src_now.shape[1]
        row_ids = top_row + jnp.arange(row_count, dtype=jnp.int32)
        pulse = wavelet[checkpoint_step + STEPS - 1 - step_index]
        source_cell = (row_ids[None, :, None] == source_depth[:, None, None]) & source_column[
            :, None, :
        ]
        injected_src = jnp.where(source_cell, pulse[:, None, None], 0.0)
        src_next = 2.0 * src_now - src_hi + velocity * laplacian[0] - velocity * injected_src
        trace_now = lax.dynamic_index_in_dim(traces, step_index, 1, keepdims=False)
        depth_table = jnp.where(
            row_ids[None, :, None] == receiver_depth[:, None, :], trace_now[:, None, :], 0.0
        )
        injected_rec = jnp.einsum(
            "szr,srx->szx",
            depth_table,
            lateral_table,
            precision=lax.Precision.HIGHEST,
            preferred_element_type=jnp.float32,
        )
        rec_next = 2.0 * rec_now - rec_hi + velocity * laplacian[1] + velocity * injected_rec
        rec_next = damper * rec_next
        return (src_next, rec_next)

    start_image = jnp.zeros(courant_sq.shape, jnp.float32)
    model = extended_2(jnp.stack([courant_sq, damping]), (("slab", 1),), 8)
    velocity_wide = model[0, 4 : slab_rows + 12]
    damper_wide = model[1, 4 : slab_rows + 12]

    def pair_step(pair_index, carry):
        src_hi, src_now, rec_hi, rec_now, image_local = carry
        step_first = 2 * pair_index
        image_local = image_local + jnp.sum(src_now * rec_now, axis=0)
        extended = extended_2(jnp.stack([src_now, rec_now, src_hi, rec_hi]), (("slab", 2),), 8)
        laplacian = laplace(extended[0:2])
        src_wide = extended[0, :, 4 : slab_rows + 12]
        rec_wide = extended[1, :, 4 : slab_rows + 12]
        src_hi_wide = extended[2, :, 4 : slab_rows + 12]
        rec_hi_wide = extended[3, :, 4 : slab_rows + 12]
        src_mid, rec_mid = advance(
            src_wide,
            src_hi_wide,
            rec_wide,
            rec_hi_wide,
            laplacian,
            velocity_wide,
            damper_wide,
            first_row - 4,
            step_first,
        )
        src_centre = src_mid[:, 4 : slab_rows + 4]
        rec_centre = rec_mid[:, 4 : slab_rows + 4]
        image_local = image_local + jnp.sum(src_centre * rec_centre, axis=0)
        second = laplace(jnp.stack([src_mid, rec_mid]))
        src_last, rec_last = advance(
            src_centre,
            src_now,
            rec_centre,
            rec_now,
            second,
            courant_sq,
            damping,
            first_row,
            step_first + 1,
        )
        return (src_centre, src_last, rec_centre, rec_last, image_local)

    carry = lax.fori_loop(
        0,
        STEPS // 2,
        pair_step,
        (source_later, source_now, receiver_later, receiver_now, start_image),
    )
    source_final = carry[1]
    receiver_final = carry[3]
    image_total = gathered_total(carry[4], "shot")
    shots_all = lax.axis_size("shot") * source_now.shape[0]
    image = image_total / math.sqrt(STEPS * shots_all)
    return (image, source_final, receiver_final)


def solution(mesh):
    in_specs = (
        P(("grp", "slab"), None),
        P(("grp", "slab"), None),
        P(("grp", "shot"), "slab", None),
        P(("grp", "shot"), "slab", None),
        P(("grp", "shot"), "slab", None),
        P(("grp", "shot"), "slab", None),
        P(("grp", "shot"), None, None),
        P("grp"),
        P(("grp", "shot")),
        P(("grp", "shot")),
        P(("grp", "shot"), None),
        P(("grp", "shot"), None),
        P(("grp", "shot")),
    )
    out_specs = (
        P(("grp", "slab"), None),
        P(("grp", "shot"), "slab", None),
        P(("grp", "shot"), "slab", None),
    )
    return jax.shard_map(local, mesh=mesh, in_specs=in_specs, out_specs=out_specs, check_vma=False)
```

profile of v0, /device:TPU:65, one launch (start us, length us, event | category | flops | bytes accessed | tf_op | source)
XLA Modules:
  0.0 340.8 jit_solution(3038531206127748717)
XLA Ops:
  9.0 6.7 %collective-permute-start.2 = (f32[2,8,1024]{2,1,0:T(8,128)S(1)}, f32[2,8,1024]{2,1,0:T(8,128)S(1)}, u32[]{:S(2)}, u32[]{:S(2)}) collective-permute-start(f32[2,8,1024]{2,1,0:T(8,128)S(1)} %get-tuple-element.729), channel_id=1, source_target_pairs={{0,1},{1,2},{2,3},{3,4},{4,5},{5,6},{6,7},{7,8},{8,9},{9,10},{10,1... | collective-permute-start | bytes 196616 | tf_op jit(solution)/shard_map/ppermute | solution.py:22
  17.2 6.0 %collective-permute-done.3 = f32[2,8,1024]{2,1,0:T(8,128)S(1)} collective-permute-done((f32[2,8,1024]{2,1,0:T(8,128)S(1)}, f32[2,8,1024]{2,1,0:T(8,128)S(1)}, u32[]{:S(2)}, u32[]{:S(2)}) %collective-permute-start.3) | collective-permute-done | bytes 65568 | tf_op jit(solution)/shard_map/ppermute | solution.py:24
  24.0 224.9 %while.26 = (s32[]{:T(128)}, f32[2,64,1024]{2,1,0:T(8,128)S(1)}, f32[2,64,1024]{2,1,0:T(8,128)S(1)}, f32[2,64,1024]{2,1,0:T(8,128)S(1)}, f32[2,64,1024]{2,1,0:T(...) while((s32[]{:T(128)}, f32[2,64,1024]{2,1,0:T(8,128)S(1)}, ...), condition=%wide.region_3.4_spmd.clone, body=%wide.region_0.3_spmd.clone.sunk | while | flops 1741394304 | bytes 51560036 | solution.py:143
  26.1 6.4 %collective-permute-start.1 = (f32[4,2,8,1024]{3,2,1,0:T(8,128)}, f32[4,2,8,1024]{3,2,1,0:T(8,128)S(1)}, u32[]{:S(2)}, u32[]{:S(2)}) collective-permute-start(f32[4,2,8,1024]{3,2,1,0:T(8,128)} %get-tuple-element.863), channel_id=1, source_target_pairs={{0,1},{1,2},{2,3},{3,4},{4,5},{5,6},{6,7},{7,8},{8,9},{9,10},{10,1... | collective-permute-start | bytes 786440 | tf_op jit(solution)/shard_map/while/body/eval_jaxpr/ppermute | solution.py:22
  40.1 3.2 fusion.118
  53.2 7.6 %collective-permute-start.1 = (f32[4,2,8,1024]{3,2,1,0:T(8,128)}, f32[4,2,8,1024]{3,2,1,0:T(8,128)S(1)}, u32[]{:S(2)}, u32[]{:S(2)}) collective-permute-start(f32[4,2,8,1024]{3,2,1,0:T(8,128)} %get-tuple-element.863), channel_id=1, source_target_pairs={{0,1},{1,2},{2,3},{3,4},{4,5},{5,6},{6,7},{7,8},{8,9},{9,10},{10,1... | collective-permute-start | bytes 786440 | tf_op jit(solution)/shard_map/while/body/eval_jaxpr/ppermute | solution.py:22
  68.4 3.2 fusion.118
  75.4 3.1 fusion.122
  81.5 8.3 %collective-permute-start.1 = (f32[4,2,8,1024]{3,2,1,0:T(8,128)}, f32[4,2,8,1024]{3,2,1,0:T(8,128)S(1)}, u32[]{:S(2)}, u32[]{:S(2)}) collective-permute-start(f32[4,2,8,1024]{3,2,1,0:T(8,128)} %get-tuple-element.863), channel_id=1, source_target_pairs={{0,1},{1,2},{2,3},{3,4},{4,5},{5,6},{6,7},{7,8},{8,9},{9,10},{10,1... | collective-permute-start | bytes 786440 | tf_op jit(solution)/shard_map/while/body/eval_jaxpr/ppermute | solution.py:22
  97.8 3.2 fusion.118
  111.0 6.0 %collective-permute-start.1 = (f32[4,2,8,1024]{3,2,1,0:T(8,128)}, f32[4,2,8,1024]{3,2,1,0:T(8,128)S(1)}, u32[]{:S(2)}, u32[]{:S(2)}) collective-permute-start(f32[4,2,8,1024]{3,2,1,0:T(8,128)} %get-tuple-element.863), channel_id=1, source_target_pairs={{0,1},{1,2},{2,3},{3,4},{4,5},{5,6},{6,7},{7,8},{8,9},{9,10},{10,1... | collective-permute-start | bytes 786440 | tf_op jit(solution)/shard_map/while/body/eval_jaxpr/ppermute | solution.py:22
  124.9 3.2 fusion.118
  131.9 3.1 fusion.122
  138.0 9.4 %collective-permute-start.1 = (f32[4,2,8,1024]{3,2,1,0:T(8,128)}, f32[4,2,8,1024]{3,2,1,0:T(8,128)S(1)}, u32[]{:S(2)}, u32[]{:S(2)}) collective-permute-start(f32[4,2,8,1024]{3,2,1,0:T(8,128)} %get-tuple-element.863), channel_id=1, source_target_pairs={{0,1},{1,2},{2,3},{3,4},{4,5},{5,6},{6,7},{7,8},{8,9},{9,10},{10,1... | collective-permute-start | bytes 786440 | tf_op jit(solution)/shard_map/while/body/eval_jaxpr/ppermute | solution.py:22
  156.8 3.2 fusion.118
  163.8 3.1 fusion.122
  170.0 5.3 %collective-permute-start.1 = (f32[4,2,8,1024]{3,2,1,0:T(8,128)}, f32[4,2,8,1024]{3,2,1,0:T(8,128)S(1)}, u32[]{:S(2)}, u32[]{:S(2)}) collective-permute-start(f32[4,2,8,1024]{3,2,1,0:T(8,128)} %get-tuple-element.863), channel_id=1, source_target_pairs={{0,1},{1,2},{2,3},{3,4},{4,5},{5,6},{6,7},{7,8},{8,9},{9,10},{10,1... | collective-permute-start | bytes 786440 | tf_op jit(solution)/shard_map/while/body/eval_jaxpr/ppermute | solution.py:22
  184.1 3.2 fusion.118
  191.1 3.1 fusion.122
  197.2 6.7 %collective-permute-start.1 = (f32[4,2,8,1024]{3,2,1,0:T(8,128)}, f32[4,2,8,1024]{3,2,1,0:T(8,128)S(1)}, u32[]{:S(2)}, u32[]{:S(2)}) collective-permute-start(f32[4,2,8,1024]{3,2,1,0:T(8,128)} %get-tuple-element.863), channel_id=1, source_target_pairs={{0,1},{1,2},{2,3},{3,4},{4,5},{5,6},{6,7},{7,8},{8,9},{9,10},{10,1... | collective-permute-start | bytes 786440 | tf_op jit(solution)/shard_map/while/body/eval_jaxpr/ppermute | solution.py:22
  212.5 3.2 fusion.118
  225.6 4.7 %collective-permute-start.1 = (f32[4,2,8,1024]{3,2,1,0:T(8,128)}, f32[4,2,8,1024]{3,2,1,0:T(8,128)S(1)}, u32[]{:S(2)}, u32[]{:S(2)}) collective-permute-start(f32[4,2,8,1024]{3,2,1,0:T(8,128)} %get-tuple-element.863), channel_id=1, source_target_pairs={{0,1},{1,2},{2,3},{3,4},{4,5},{5,6},{6,7},{7,8},{8,9},{9,10},{10,1... | collective-permute-start | bytes 786440 | tf_op jit(solution)/shard_map/while/body/eval_jaxpr/ppermute | solution.py:22
  237.9 3.2 fusion.118
  249.0 81.7 %all-gather.3.cloned.1.call-done = f32[1024,1024]{1,0:T(8,128)} async-done(((f32[64,1024]{1,0:T(8,128)}), f32[1024,1024]{1,0:T(8,128)}) %all-gather.3.cloned.1.call-update) | async-done | bytes 4194320 | tf_op jit(solution)/shard_map/all_gather | solution.py:32
  (411 shorter events, 138.2 us)
Async XLA Ops:
  7.2 323.5 %all-gather.3.cloned.1.call-start = ((), (), s32[]{:S(2)}) async-start(), calls=%async_computation | async-start | bytes 4456448 | tf_op jit(solution)/shard_map/all_gather | solution.py:32
  8.2 15.7 %copy-start.6 = (f32[2,64,1024]{2,1,0:T(8,128)S(1)}, f32[2,64,1024]{2,1,0:T(8,128)}, u32[]{:S(2)}) copy-start(f32[2,64,1024]{2,1,0:T(8,128)} %param.19) | copy-start | bytes 1572868
  9.0 15.0 %copy-start.14 = (s32[2]{0:T(128)S(1)}, s32[2]{0:T(128)}, u32[]{:S(2)}) copy-start(s32[2]{0:T(128)} %param.27) | copy-start | bytes 28
  9.0 15.0 %copy-start.15 = (s32[2]{0:T(128)S(1)}, s32[2]{0:T(128)}, u32[]{:S(2)}) copy-start(s32[2]{0:T(128)} %param.24) | copy-start | bytes 28
  9.0 8.1 %collective-permute-start.2 = (f32[2,8,1024]{2,1,0:T(8,128)S(1)}, f32[2,8,1024]{2,1,0:T(8,128)S(1)}, u32[]{:S(2)}, u32[]{:S(2)}) collective-permute-start(f32[2,8,1024]{2,1,0:T(8,128)S(1)} %get-tuple-element.729), channel_id=1, source_target_pairs={{0,1},{1,2},{2,3},{3,4},{4,5},{5,6},{6,7},{7,8},{8,9},{9,10},{10,1... | collective-permute-start | bytes 196616 | tf_op jit(solution)/shard_map/ppermute | solution.py:22
  15.7 7.4 %collective-permute-start.3 = (f32[2,8,1024]{2,1,0:T(8,128)S(1)}, f32[2,8,1024]{2,1,0:T(8,128)S(1)}, u32[]{:S(2)}, u32[]{:S(2)}) collective-permute-start(f32[2,8,1024]{2,1,0:T(8,128)S(1)} %get-tuple-element.730), channel_id=1, source_target_pairs={{1,0},{2,1},{3,2},{4,3},{5,4},{6,5},{7,6},{8,7},{9,8},{10,9},{11,1... | collective-permute-start | bytes 196616 | tf_op jit(solution)/shard_map/ppermute | solution.py:24
  24.8 9.8 %collective-permute-start = (f32[4,2,8,1024]{3,2,1,0:T(8,128)}, f32[4,2,8,1024]{3,2,1,0:T(8,128)S(1)}, u32[]{:S(2)}, u32[]{:S(2)}) collective-permute-start(f32[4,2,8,1024]{3,2,1,0:T(8,128)} %get-tuple-element.862), channel_id=1, source_target_pairs={{1,0},{2,1},{3,2},{4,3},{5,4},{6,5},{7,6},{8,7},{9,8},{10,9},{11,1... | collective-permute-start | bytes 786440 | tf_op jit(solution)/shard_map/while/body/eval_jaxpr/ppermute | solution.py:24
  26.1 10.0 %collective-permute-start.1 = (f32[4,2,8,1024]{3,2,1,0:T(8,128)}, f32[4,2,8,1024]{3,2,1,0:T(8,128)S(1)}, u32[]{:S(2)}, u32[]{:S(2)}) collective-permute-start(f32[4,2,8,1024]{3,2,1,0:T(8,128)} %get-tuple-element.863), channel_id=1, source_target_pairs={{0,1},{1,2},{2,3},{3,4},{4,5},{5,6},{6,7},{7,8},{8,9},{9,10},{10,1... | collective-permute-start | bytes 786440 | tf_op jit(solution)/shard_map/while/body/eval_jaxpr/ppermute | solution.py:22
  51.9 11.0 %collective-permute-start = (f32[4,2,8,1024]{3,2,1,0:T(8,128)}, f32[4,2,8,1024]{3,2,1,0:T(8,128)S(1)}, u32[]{:S(2)}, u32[]{:S(2)}) collective-permute-start(f32[4,2,8,1024]{3,2,1,0:T(8,128)} %get-tuple-element.862), channel_id=1, source_target_pairs={{1,0},{2,1},{3,2},{4,3},{5,4},{6,5},{7,6},{8,7},{9,8},{10,9},{11,1... | collective-permute-start | bytes 786440 | tf_op jit(solution)/shard_map/while/body/eval_jaxpr/ppermute | solution.py:24
  53.2 11.2 %collective-permute-start.1 = (f32[4,2,8,1024]{3,2,1,0:T(8,128)}, f32[4,2,8,1024]{3,2,1,0:T(8,128)S(1)}, u32[]{:S(2)}, u32[]{:S(2)}) collective-permute-start(f32[4,2,8,1024]{3,2,1,0:T(8,128)} %get-tuple-element.863), channel_id=1, source_target_pairs={{0,1},{1,2},{2,3},{3,4},{4,5},{5,6},{6,7},{7,8},{8,9},{9,10},{10,1... | collective-permute-start | bytes 786440 | tf_op jit(solution)/shard_map/while/body/eval_jaxpr/ppermute | solution.py:22
  80.2 12.6 %collective-permute-start = (f32[4,2,8,1024]{3,2,1,0:T(8,128)}, f32[4,2,8,1024]{3,2,1,0:T(8,128)S(1)}, u32[]{:S(2)}, u32[]{:S(2)}) collective-permute-start(f32[4,2,8,1024]{3,2,1,0:T(8,128)} %get-tuple-element.862), channel_id=1, source_target_pairs={{1,0},{2,1},{3,2},{4,3},{5,4},{6,5},{7,6},{8,7},{9,8},{10,9},{11,1... | collective-permute-start | bytes 786440 | tf_op jit(solution)/shard_map/while/body/eval_jaxpr/ppermute | solution.py:24
  81.5 12.3 %collective-permute-start.1 = (f32[4,2,8,1024]{3,2,1,0:T(8,128)}, f32[4,2,8,1024]{3,2,1,0:T(8,128)S(1)}, u32[]{:S(2)}, u32[]{:S(2)}) collective-permute-start(f32[4,2,8,1024]{3,2,1,0:T(8,128)} %get-tuple-element.863), channel_id=1, source_target_pairs={{0,1},{1,2},{2,3},{3,4},{4,5},{5,6},{6,7},{7,8},{8,9},{9,10},{10,1... | collective-permute-start | bytes 786440 | tf_op jit(solution)/shard_map/while/body/eval_jaxpr/ppermute | solution.py:22
  109.7 10.3 %collective-permute-start = (f32[4,2,8,1024]{3,2,1,0:T(8,128)}, f32[4,2,8,1024]{3,2,1,0:T(8,128)S(1)}, u32[]{:S(2)}, u32[]{:S(2)}) collective-permute-start(f32[4,2,8,1024]{3,2,1,0:T(8,128)} %get-tuple-element.862), channel_id=1, source_target_pairs={{1,0},{2,1},{3,2},{4,3},{5,4},{6,5},{7,6},{8,7},{9,8},{10,9},{11,1... | collective-permute-start | bytes 786440 | tf_op jit(solution)/shard_map/while/body/eval_jaxpr/ppermute | solution.py:24
  111.0 10.0 %collective-permute-start.1 = (f32[4,2,8,1024]{3,2,1,0:T(8,128)}, f32[4,2,8,1024]{3,2,1,0:T(8,128)S(1)}, u32[]{:S(2)}, u32[]{:S(2)}) collective-permute-start(f32[4,2,8,1024]{3,2,1,0:T(8,128)} %get-tuple-element.863), channel_id=1, source_target_pairs={{0,1},{1,2},{2,3},{3,4},{4,5},{5,6},{6,7},{7,8},{8,9},{9,10},{10,1... | collective-permute-start | bytes 786440 | tf_op jit(solution)/shard_map/while/body/eval_jaxpr/ppermute | solution.py:22
  136.7 15.1 %collective-permute-start = (f32[4,2,8,1024]{3,2,1,0:T(8,128)}, f32[4,2,8,1024]{3,2,1,0:T(8,128)S(1)}, u32[]{:S(2)}, u32[]{:S(2)}) collective-permute-start(f32[4,2,8,1024]{3,2,1,0:T(8,128)} %get-tuple-element.862), channel_id=1, source_target_pairs={{1,0},{2,1},{3,2},{4,3},{5,4},{6,5},{7,6},{8,7},{9,8},{10,9},{11,1... | collective-permute-start | bytes 786440 | tf_op jit(solution)/shard_map/while/body/eval_jaxpr/ppermute | solution.py:24
  138.0 14.8 %collective-permute-start.1 = (f32[4,2,8,1024]{3,2,1,0:T(8,128)}, f32[4,2,8,1024]{3,2,1,0:T(8,128)S(1)}, u32[]{:S(2)}, u32[]{:S(2)}) collective-permute-start(f32[4,2,8,1024]{3,2,1,0:T(8,128)} %get-tuple-element.863), channel_id=1, source_target_pairs={{0,1},{1,2},{2,3},{3,4},{4,5},{5,6},{6,7},{7,8},{8,9},{9,10},{10,1... | collective-permute-start | bytes 786440 | tf_op jit(solution)/shard_map/while/body/eval_jaxpr/ppermute | solution.py:22
  168.6 10.5 %collective-permute-start = (f32[4,2,8,1024]{3,2,1,0:T(8,128)}, f32[4,2,8,1024]{3,2,1,0:T(8,128)S(1)}, u32[]{:S(2)}, u32[]{:S(2)}) collective-permute-start(f32[4,2,8,1024]{3,2,1,0:T(8,128)} %get-tuple-element.862), channel_id=1, source_target_pairs={{1,0},{2,1},{3,2},{4,3},{5,4},{6,5},{7,6},{8,7},{9,8},{10,9},{11,1... | collective-permute-start | bytes 786440 | tf_op jit(solution)/shard_map/while/body/eval_jaxpr/ppermute | solution.py:24
  170.0 10.2 %collective-permute-start.1 = (f32[4,2,8,1024]{3,2,1,0:T(8,128)}, f32[4,2,8,1024]{3,2,1,0:T(8,128)S(1)}, u32[]{:S(2)}, u32[]{:S(2)}) collective-permute-start(f32[4,2,8,1024]{3,2,1,0:T(8,128)} %get-tuple-element.863), channel_id=1, source_target_pairs={{0,1},{1,2},{2,3},{3,4},{4,5},{5,6},{6,7},{7,8},{8,9},{9,10},{10,1... | collective-permute-start | bytes 786440 | tf_op jit(solution)/shard_map/while/body/eval_jaxpr/ppermute | solution.py:22
  195.9 11.6 %collective-permute-start = (f32[4,2,8,1024]{3,2,1,0:T(8,128)}, f32[4,2,8,1024]{3,2,1,0:T(8,128)S(1)}, u32[]{:S(2)}, u32[]{:S(2)}) collective-permute-start(f32[4,2,8,1024]{3,2,1,0:T(8,128)} %get-tuple-element.862), channel_id=1, source_target_pairs={{1,0},{2,1},{3,2},{4,3},{5,4},{6,5},{7,6},{8,7},{9,8},{10,9},{11,1... | collective-permute-start | bytes 786440 | tf_op jit(solution)/shard_map/while/body/eval_jaxpr/ppermute | solution.py:24
  197.2 11.3 %collective-permute-start.1 = (f32[4,2,8,1024]{3,2,1,0:T(8,128)}, f32[4,2,8,1024]{3,2,1,0:T(8,128)S(1)}, u32[]{:S(2)}, u32[]{:S(2)}) collective-permute-start(f32[4,2,8,1024]{3,2,1,0:T(8,128)} %get-tuple-element.863), channel_id=1, source_target_pairs={{0,1},{1,2},{2,3},{3,4},{4,5},{5,6},{6,7},{7,8},{8,9},{9,10},{10,1... | collective-permute-start | bytes 786440 | tf_op jit(solution)/shard_map/while/body/eval_jaxpr/ppermute | solution.py:22
  224.3 8.4 %collective-permute-start = (f32[4,2,8,1024]{3,2,1,0:T(8,128)}, f32[4,2,8,1024]{3,2,1,0:T(8,128)S(1)}, u32[]{:S(2)}, u32[]{:S(2)}) collective-permute-start(f32[4,2,8,1024]{3,2,1,0:T(8,128)} %get-tuple-element.862), channel_id=1, source_target_pairs={{1,0},{2,1},{3,2},{4,3},{5,4},{6,5},{7,6},{8,7},{9,8},{10,9},{11,1... | collective-permute-start | bytes 786440 | tf_op jit(solution)/shard_map/while/body/eval_jaxpr/ppermute | solution.py:24
  225.6 8.3 %collective-permute-start.1 = (f32[4,2,8,1024]{3,2,1,0:T(8,128)}, f32[4,2,8,1024]{3,2,1,0:T(8,128)S(1)}, u32[]{:S(2)}, u32[]{:S(2)}) collective-permute-start(f32[4,2,8,1024]{3,2,1,0:T(8,128)} %get-tuple-element.863), channel_id=1, source_target_pairs={{0,1},{1,2},{2,3},{3,4},{4,5},{5,6},{6,7},{7,8},{8,9},{9,10},{10,1... | collective-permute-start | bytes 786440 | tf_op jit(solution)/shard_map/while/body/eval_jaxpr/ppermute | solution.py:22
  248.9 84.3 %copy-start.2 = (f32[2,64,1024]{2,1,0:T(8,128)}, f32[2,64,1024]{2,1,0:T(8,128)S(1)}, u32[]{:S(2)}) copy-start(f32[2,64,1024]{2,1,0:T(8,128)S(1)} %get-tuple-element.960) | copy-start | bytes 1572868
  248.9 84.3 %copy-start.4 = (f32[2,64,1024]{2,1,0:T(8,128)}, f32[2,64,1024]{2,1,0:T(8,128)S(1)}, u32[]{:S(2)}) copy-start(f32[2,64,1024]{2,1,0:T(8,128)S(1)} %get-tuple-element.962) | copy-start | bytes 1572868
  (89 other events, 212.4 us)
Sparse Core Ops, SparseCore 0:
  249.1 81.5 all-gather.2
where the time goes:
time: 342 us; the launch traced here: 341 us
  waiting for transfers between devices  105 us (31%)
  starting transfers between devices  72.9 us (21%)
  other arithmetic  65.4 us (19%)
  matrix products  50.3 us (15%)
  local copies, waits for them, and re-layouts  31.5 us (9%)
  between operations  14.3 us (4%)
    all_gather x1, waiting for transfers between devices, gathered_total(): blocks = lax.all_gather(shard, axis)  81.7 us
    ppermute x9, starting transfers between devices, extended_2(): lax.ppermute(tail, axis, [(i, (i + 1) % count) for i in range(ends)])  61.1 us
    dot_general x16, matrix products, advance(): jnp.einsum('szr,srx->szx', depth_table, lateral_table, precision=lax.Prec...  50.3 us
    add x16, other arithmetic, laplace(): result + stencil_coeffs[offset] * (extended[..., 4 + offset:4 + offset +...  39.8 us
    while x160, local copies, waits for them, and re-layouts  18.2 us
    ppermute x9, waiting for transfers between devices, extended_2(): lax.ppermute(head, axis, [((i + 1) % count, i) for i in range(ends)])  13.5 us
    ppermute x9, starting transfers between devices, extended_2(): lax.ppermute(head, axis, [((i + 1) % count, i) for i in range(ends)])  11.7 us
    gather x16, local copies, waits for them, and re-layouts, advance(): pulse = wavelet[checkpoint_step + STEPS - 1 - step_index]  10.2 us
  transfers between devices with their start and end apart: 19, of which 16 were waited for; matrix products, arithmetic and copies ran while one was open for 4% of the time, Pallas kernels for 0%

commit v1 on v0

v1 whole, which is shorter than its diff:
```python
import functools
import math

import jax
import jax.numpy as jnp
from jax import lax
from jax.experimental import pallas as pl
from jax.experimental.pallas import tpu as pltpu
from jax.sharding import PartitionSpec as P

MESH = pl.DeviceIdType.MESH
F32 = jnp.float32
BF16 = jnp.bfloat16

C0, C1, C2, C3, C4 = (-205.0 / 72.0, 8.0 / 5.0, -1.0 / 5.0, 8.0 / 315.0, -1.0 / 560.0)

OWN = slice(4, 12)


def rows(start, count=8):
    return pl.ds(start, count)


def kernel(
    steps,
    courant,
    sponge,
    src_hi,
    src_now,
    rec_hi,
    rec_now,
    traces,
    rec_depth,
    rec_lateral,
    wavelet,
    src_depth,
    src_lateral,
    start_step,
    image_out,
    src_out,
    rec_out,
    N,
    M,
    V,
    D,
    AS,
    VS,
    AR,
    VR,
    G,
    IA,
    IB,
    W,
    DP,
    T,
    CORR,
    PAIR,
    HALF,
    PARTS,
    FIN,
    IMG,
    n_send,
    n_recv,
    h_send,
    h_recv,
    c_send,
    c_recv,
    pair_send,
    pair_recv,
    rs_send,
    rs_recv,
    ag_send,
    ag_recv,
):
    slab, slabs = lax.axis_index("slab"), lax.axis_size("slab")
    me, members = lax.axis_index("shot"), lax.axis_size("shot")
    chips = members // 2
    chip, core = me // 2, lax.rem(me, 2)
    depth = courant.shape[0]
    shots = src_now.shape[0]
    nrec = traces.shape[2]
    blocks = steps // 2
    wide = depth + 8
    first = slab * depth
    has_up, has_down = slab > 0, slab < slabs - 1
    part = depth // chips
    planes = 2 * shots

    barrier = pltpu.get_barrier_semaphore()

    def greet(target):
        pl.semaphore_signal(barrier, inc=1, device_id=target, device_id_type=MESH)

    @pl.when(has_up)
    def _():
        greet({"slab": slab - 1})

    @pl.when(has_down)
    def _():
        greet({"slab": slab + 1})

    partner = chip * 2 + (1 - core)
    greet({"shot": partner})
    peers = [lax.rem(chip + d, chips) * 2 + core for d in range(1, chips)]
    for peer in peers:
        greet({"shot": peer})

    lane = lax.broadcasted_iota(jnp.int32, (4, 8, 128), 2)
    lane8 = lax.broadcasted_iota(jnp.int32, (8, 8, 128), 2)
    reg8 = lax.broadcasted_iota(jnp.int32, (8, 8, 128), 0)
    row8 = lax.broadcasted_iota(jnp.int32, (8, 8, 128), 1)
    cell8 = 8 * lane8 + reg8

    def up_lane(v):
        return jnp.where(lane == 0, 0.0, pltpu.roll(v, 1, axis=2))

    def down_lane(v):
        return jnp.where(lane == 127, 0.0, pltpu.roll(v, 127, axis=2))

    def to_registers(block, slot, put):
        for t in range(8):
            T[slot, 128 * t : 128 * (t + 1), :] = block(t).T
        for r in range(8):
            put(r, T[slot, pl.ds(r, 128, stride=8), :].T)

    def field_block(ref):
        return lambda t: ref[:, :, 128 * t : 128 * (t + 1)].reshape(shots * depth, 128)

    def put_now(field):
        def put(r, value):
            for s in range(shots):
                v = value[depth * s : depth * (s + 1)]
                N[0, 2 * s + field, 4 + r, 8 : 8 + depth, :] = v
                edge = lax.broadcasted_iota(jnp.int32, (depth, 128), 1)
                if r < 4:
                    N[0, 2 * s + field, 12 + r, 8 : 8 + depth, :] = jnp.where(
                        edge == 127, 0.0, pltpu.roll(v, 127, axis=1)
                    )
                else:
                    N[0, 2 * s + field, r - 4, 8 : 8 + depth, :] = jnp.where(
                        edge == 0, 0.0, pltpu.roll(v, 1, axis=1)
                    )

        return put

    def put_hi(field):
        def put(r, value):
            for s in range(shots):
                M[2 * s + field, 4 + r, 4 : 4 + depth, :] = value[depth * s : depth * (s + 1)]

        return put

    def model_block(t):
        cols = slice(128 * t, 128 * (t + 1))
        return jnp.concatenate(
            [courant[:, cols], 1.0 - 0.06 * sponge[:, cols].astype(F32)], axis=0
        )

    def put_model(r, value):
        V[r, 4 : 4 + depth, :] = value[:depth]
        D[r, 4 : 4 + depth, :] = value[depth:]

    zeros = jnp.zeros((8, 8, 128), F32)

    def clear(now_row, row):
        for p in range(planes):
            for slot in range(2):
                N[slot, p, OWN, rows(now_row), :] = zeros
            M[p, OWN, rows(row), :] = zeros
        for ref in (V, D):
            ref[:, rows(row), :] = zeros

    @pl.when(slab == 0)
    def _():
        clear(0, 0)

    @pl.when(slab == slabs - 1)
    def _():
        clear(8 + depth, depth)

    to_registers(field_block(src_now), 0, put_now(0))
    to_registers(field_block(src_hi), 1, put_hi(0))
    to_registers(field_block(rec_now), 0, put_now(1))
    to_registers(field_block(rec_hi), 1, put_hi(1))
    to_registers(model_block, 0, put_model)

    def shift(ref_at, src_row, dst_row, count, send, recv, to):
        return pltpu.make_async_remote_copy(
            src_ref=ref_at(src_row, count),
            dst_ref=ref_at(dst_row, count),
            send_sem=send,
            recv_sem=recv,
            device_id={"slab": to},
            device_id_type=MESH,
        )

    def now_copy(slot, p, direction):
        at = lambda row, count: N.at[slot, p, OWN, pl.ds(row, count), :]
        if direction == 0:
            return shift(at, 8, 8 + depth, 8, n_send.at[p, 0], n_recv.at[slot, p, 0], slab - 1)
        return shift(at, depth, 0, 8, n_send.at[p, 1], n_recv.at[slot, p, 1], slab + 1)

    def hi_copy(p, direction):
        at = lambda row, count: M.at[p, OWN, pl.ds(row, count), :]
        if direction == 0:
            return shift(at, 4, 4 + depth, 4, h_send.at[p, 0], h_recv.at[p, 0], slab - 1)
        return shift(at, depth, 0, 4, h_send.at[p, 1], h_recv.at[p, 1], slab + 1)

    def model_copy(which, direction):
        ref = (V, D)[which]
        at = lambda row, count: ref.at[:, pl.ds(row, count), :]
        sems = c_send.at[which, direction], c_recv.at[which, direction]
        if direction == 0:
            return shift(at, 4, 4 + depth, 4, *sems, slab - 1)
        return shift(at, depth, 0, 4, *sems, slab + 1)

    def each_way(act):
        @pl.when(has_up)
        def _():
            act(0, 1)

        @pl.when(has_down)
        def _():
            act(1, 0)

    greeted = (
        has_up.astype(jnp.int32) + has_down.astype(jnp.int32) + len(peers) + 1
    )
    pl.semaphore_wait(barrier, greeted)

    def send_first(out, _):
        model_copy(0, out).start()
        model_copy(1, out).start()
        for p in range(planes):
            hi_copy(p, out).start()
            now_copy(0, p, out).start()

    each_way(send_first)

    pad = 16 * ((wide + 15) // 16)
    top = 2 * pad

    rec_ids = first - 4 + lax.broadcasted_iota(jnp.int32, (wide, nrec), 0)
    for s in range(shots):
        DP[s] = (rec_ids == rec_depth[s : s + 1, :]).astype(F32)
        for q in range(nrec // 128):
            wanted = jnp.broadcast_to(
                rec_lateral[s : s + 1, 128 * q : 128 * (q + 1)].astype(F32), (128, 128)
            ).T
            at = lax.broadcasted_iota(jnp.int32, (128, 128), 1).astype(F32) * 8.0
            for r in range(8):
                W[s, 128 * q : 128 * (q + 1), 128 * r : 128 * (r + 1)] = (
                    (wanted == at + float(r)).astype(F32).astype(BF16)
                )

    def inject(s, block):
        def terms(step):
            t = traces[s, pl.ds(step, 1), :] * (1.0 / C1)
            hi = t.astype(BF16).astype(F32)
            return hi, t - hi

        gap = jnp.zeros((pad - wide, nrec), F32)
        table = []
        for term in terms(2 * block):
            table += [DP[s] * term, gap]
        for term in terms(2 * block + 1):
            table += [DP[s, 4 : 4 + depth, :] * term]
        table = jnp.concatenate(table, axis=0).astype(BF16)
        for c in range(4):
            got = jnp.dot(
                table, W[s, :, 256 * c : 256 * (c + 1)], preferred_element_type=F32
            )
            a = got[0:wide] + got[pad : pad + wide]
            b = got[top : top + depth] + got[top + depth : top + 2 * depth]
            for e in range(2):
                IA[s, 2 * c + e] = a[:, 128 * e : 128 * (e + 1)]
                IB[s, 2 * c + e] = b[:, 128 * e : 128 * (e + 1)]

    def coefficients(m):
        at = rows(m)
        v, d = V[:, at, :], D[:, at, :]
        a = 2.0 + (2.0 * C0) * v
        AS[:, at, :] = a
        AR[:, at, :] = d * a
        VS[:, at, :] = C1 * v
        VR[:, at, :] = (C1 * d) * v
        for s in range(shots):
            hit = (cell8 == src_lateral[s]) & (row8 + (first - 4 + m) == src_depth[s])
            G[s, :, at, :] = jnp.where(hit, -v, 0.0)

    def spread(X, z):
        total = None
        for k, a in ((1, None), (2, C2 / C1), (3, C3 / C1), (4, C4 / C1)):
            pair = (X(4 + k) + X(4 - k)) + (z(k) + z(-k))
            total = pair if a is None else total + a * pair
        return total

    def neighbours(ref, pre, row, stored):
        z = lambda k: ref[pre + (OWN, rows(row + k), slice(None))]
        if stored:
            X = lambda k: ref[pre + (slice(k, k + 8), rows(row), slice(None))]
            return X, z
        c = z(0)
        wide_c = jnp.concatenate([up_lane(c[4:]), c, down_lane(c[:4])], axis=0)
        return (lambda k: wide_c[k : k + 8]), z

    def advance(field, s, centre, total, hi, m, injected, pulse):
        at = rows(m)
        if field == 0:
            return AS[:, at, :] * centre - hi + (VS[:, at, :] * total + pulse * G[s, :, at, :])
        return AR[:, at, :] * centre - D[:, at, :] * hi + VR[:, at, :] * (total + injected)

    def put_field(ref, pre, row, value):
        at = rows(row)
        ref[pre + (OWN, at, slice(None))] = value
        ref[pre + (slice(12, 16), at, slice(None))] = down_lane(value[:4])
        ref[pre + (slice(0, 4), at, slice(None))] = up_lane(value[4:])

    def first_step(slot, s, field, g, pulse, stored):
        p, m = 2 * s + field, 8 * g
        X, z = neighbours(N, (slot, p), m + 4, stored)
        injected = IA[s, :, rows(m), :] if field else None
        new = advance(field, s, z(0), spread(X, z), M[p, OWN, rows(m), :], m, injected, pulse)
        put_field(M, (p,), m, new)

    def second_step(slot, to, s, field, g, pulse, final=False):
        p, m = 2 * s + field, 8 * g + 4
        X, z = neighbours(M, (p,), m, True)
        injected = IB[s, :, rows(8 * g), :] if field else None
        hi = N[slot, p, OWN, rows(8 * g + 8), :]
        centre = z(0)
        new = advance(field, s, centre, spread(X, z), hi, m, injected, pulse)
        if final:
            N[to, p, OWN, rows(8 * g + 8), :] = new
        else:
            put_field(N, (to, p), 8 * g + 8, new)
            if field:
                CORR[:, rows(8 * g), :] += (
                    N[slot, p - 1, OWN, rows(8 * g + 8), :] * hi
                    + M[p - 1, OWN, rows(m), :] * centre
                )

    groups = depth // 8

    def pulse_of(s, step):
        return wavelet[start_step[s] + steps - 1 - step]

    for g in range(1, groups):
        coefficients(8 * g)
    for g in range(groups):
        CORR[:, rows(8 * g), :] = zeros
    for s in range(shots):
        inject(s, 0)
        for field in range(2):
            pulse = pulse_of(s, 0)
            for g in range(1, groups):
                first_step(0, s, field, g, pulse, True)

    def arrive_first(out, inn):
        for which in range(2):
            model_copy(which, out).wait_send()
            model_copy(which, inn).wait_recv()

    def arrive_hi(p):
        def act(out, inn):
            hi_copy(p, out).wait_send()
            hi_copy(p, inn).wait_recv()

        return act

    def arrive_now(slot, p):
        def act(out, inn):
            now_copy(slot, p, out).wait_send()
            now_copy(slot, p, inn).wait_recv()

        return act

    def send_now(slot, p):
        def act(out, _):
            now_copy(slot, p, out).start()

        return act

    each_way(arrive_first)
    coefficients(0)
    coefficients(8 * groups)
    for p in range(planes):
        each_way(arrive_hi(p))

    def block(b, carry):
        slot = lax.rem(b, 2)
        to = 1 - slot
        for s in range(shots):
            pulses = [pulse_of(s, 2 * b + j) for j in range(3)]
            for field in range(2):
                p = 2 * s + field
                each_way(arrive_now(slot, p))
                for g in (0, groups):
                    first_step(slot, s, field, g, pulses[0], False)
                for g in (0, groups - 1):
                    second_step(slot, to, s, field, g, pulses[1])
                each_way(send_now(to, p))
            for field in range(2):
                for g in range(1, groups - 1):
                    second_step(slot, to, s, field, g, pulses[1])
            inject(s, b + 1)
            for field in range(2):
                for g in range(1, groups):
                    first_step(to, s, field, g, pulses[2], True)
        return carry

    lax.fori_loop(0, blocks - 1, block, 0)

    last = blocks - 1
    slot = last % 2
    to = 1 - slot
    for s in range(shots):
        for field in range(2):
            p = 2 * s + field
            each_way(arrive_now(slot, p))
            for g in (0, groups):
                first_step(slot, s, field, g, pulse_of(s, 2 * last), False)
    for g in range(groups):
        total = CORR[:, rows(8 * g), :]
        for s in range(shots):
            at = rows(8 * g + 8)
            total = total + N[slot, 2 * s, OWN, at, :] * N[slot, 2 * s + 1, OWN, at, :]
            at = rows(8 * g + 4)
            total = total + M[2 * s, OWN, at, :] * M[2 * s + 1, OWN, at, :]
        CORR[:, rows(8 * g), :] = total

    def remote(src, dst, send, recv, shot):
        return pltpu.make_async_remote_copy(
            src_ref=src,
            dst_ref=dst,
            send_sem=send,
            recv_sem=recv,
            device_id={"shot": shot},
            device_id_type=MESH,
        )

    mine = pl.ds(4 * core, 4)
    pair = remote(CORR.at[pl.ds(4 * (1 - core), 4)], PAIR, pair_send.at[0], pair_recv.at[0], partner)
    pair.start()
    for s in range(shots):
        for field in range(2):
            for g in range(groups // 2):
                second_step(slot, to, s, field, g, pulse_of(s, steps - 1), True)
    pair.wait()
    HALF[...] = CORR[mine] + PAIR[...]

    def scatter(d):
        other = lax.rem(chip + d, chips)
        return remote(
            HALF.at[:, pl.ds(other * part, part), :],
            PARTS.at[chips - d],
            rs_send.at[d],
            rs_recv.at[chips - d],
            other * 2 + core,
        )

    def scattered(d):
        return remote(HALF.at[:, pl.ds(0, part), :], PARTS.at[d], rs_send.at[d], rs_recv.at[d], partner)

    order = sorted(range(1, chips), key=lambda d: -min(d, chips - d))
    for d in order:
        scatter(d).start()
    for s in range(shots):
        for field in range(2):
            for g in range(groups // 2, groups):
                second_step(slot, to, s, field, g, pulse_of(s, steps - 1), True)

    def from_registers(get, count, slot, put):
        for r in range(8):
            T[slot, pl.ds(r, 128, stride=8), 0:count] = get(r).T
        for t in range(8):
            put(t, T[slot, 128 * t : 128 * (t + 1), 0:count].T)

    def field_out(field, ref):
        def get(r):
            return jnp.concatenate(
                [N[to, 2 * s + field, 4 + r, 8 : 8 + depth, :] for s in range(shots)], axis=0
            )

        def put(t, value):
            for s in range(shots):
                ref[s, :, 128 * t : 128 * (t + 1)] = value[depth * s : depth * (s + 1)]

        from_registers(get, shots * depth, field, put)

    field_out(0, src_out)
    for d in order:
        scattered(d).wait_recv()
    total = HALF[:, pl.ds(chip * part, part), :]
    for d in range(1, chips):
        total = total + PARTS[d]
    FIN[...] = total * (1.0 / math.sqrt(steps * shots * members))

    def gather(d):
        other = lax.rem(chip + d, chips)
        return remote(
            FIN,
            IMG.at[mine, pl.ds(chip * part, part), :],
            ag_send.at[d],
            ag_recv.at[chips - d],
            other * 2 + core,
        )

    def gathered(d):
        other = lax.rem(chip + d, chips)
        return remote(
            FIN,
            IMG.at[mine, pl.ds(other * part, part), :],
            ag_send.at[d],
            ag_recv.at[d],
            partner,
        )

    for d in order:
        gather(d).start()
    IMG[mine, pl.ds(chip * part, part), :] = FIN[...]
    field_out(1, rec_out)
    for d in order:
        gathered(d).wait_recv()
    swap = remote(IMG.at[mine], IMG.at[mine], pair_send.at[1], pair_recv.at[1], partner)
    swap.start()
    for d in range(1, chips):
        scatter(d).wait_send()
        gather(d).wait_send()
    swap.wait()

    def image_put(t, value):
        image_out[:, 128 * t : 128 * (t + 1)] = value

    from_registers(lambda r: IMG[r], depth, 0, image_put)


def local(
    courant_sq,
    sponge_level,
    source_later,
    source_now,
    receiver_later,
    receiver_now,
    traces,
    wavelet,
    source_depth,
    source_lateral,
    receiver_depth,
    receiver_lateral,
    checkpoint_step,
):
    depth, lateral = courant_sq.shape
    shots, steps, nrec = traces.shape
    members = lax.axis_size("shot")
    chips = members // 2
    part = depth // chips
    wide = depth + 8
    planes = 2 * shots
    vmem = pl.BlockSpec(memory_space=pltpu.VMEM)
    smem = pl.BlockSpec(memory_space=pltpu.SMEM)
    return pl.pallas_call(
        functools.partial(kernel, steps),
        name="rtm_window",
        out_shape=(
            jax.ShapeDtypeStruct((depth, lateral), F32),
            jax.ShapeDtypeStruct((shots, depth, lateral), F32),
            jax.ShapeDtypeStruct((shots, depth, lateral), F32),
        ),
        in_specs=[vmem] * 9 + [smem] * 4,
        out_specs=(vmem, vmem, vmem),
        scratch_shapes=[
            pltpu.VMEM((2, planes, 16, depth + 16, 128), F32),
            pltpu.VMEM((planes, 16, wide, 128), F32),
            *[pltpu.VMEM((8, wide, 128), F32) for _ in range(6)],
            pltpu.VMEM((shots, 8, wide, 128), F32),
            pltpu.VMEM((shots, 8, wide, 128), F32),
            pltpu.VMEM((shots, 8, depth, 128), F32),
            pltpu.VMEM((shots, nrec, lateral), BF16),
            pltpu.VMEM((shots, wide, nrec), F32),
            pltpu.VMEM((2, lateral, 128), F32),
            pltpu.VMEM((8, depth, 128), F32),
            pltpu.VMEM((4, depth, 128), F32),
            pltpu.VMEM((4, depth, 128), F32),
            pltpu.VMEM((chips, 4, part, 128), F32),
            pltpu.VMEM((4, part, 128), F32),
            pltpu.VMEM((8, depth, 128), F32),
            pltpu.SemaphoreType.DMA((planes, 2)),
            pltpu.SemaphoreType.DMA((2, planes, 2)),
            pltpu.SemaphoreType.DMA((planes, 2)),
            pltpu.SemaphoreType.DMA((planes, 2)),
            pltpu.SemaphoreType.DMA((2, 2)),
            pltpu.SemaphoreType.DMA((2, 2)),
            pltpu.SemaphoreType.DMA((2,)),
            pltpu.SemaphoreType.DMA((2,)),
            pltpu.SemaphoreType.DMA((chips,)),
            pltpu.SemaphoreType.DMA((chips,)),
            pltpu.SemaphoreType.DMA((chips,)),
            pltpu.SemaphoreType.DMA((chips,)),
        ],
        compiler_params=pltpu.CompilerParams(collective_id=0, has_side_effects=True),
    )(
        courant_sq,
        sponge_level,
        source_later,
        source_now,
        receiver_later,
        receiver_now,
        traces,
        receiver_depth,
        receiver_lateral,
        wavelet,
        source_depth,
        source_lateral,
        checkpoint_step,
    )


def solution(mesh):
    in_specs = (
        P(("grp", "slab"), None),
        P(("grp", "slab"), None),
        P(("grp", "shot"), "slab", None),
        P(("grp", "shot"), "slab", None),
        P(("grp", "shot"), "slab", None),
        P(("grp", "shot"), "slab", None),
        P(("grp", "shot"), None, None),
        P("grp"),
        P(("grp", "shot")),
        P(("grp", "shot")),
        P(("grp", "shot"), None),
        P(("grp", "shot"), None),
        P(("grp", "shot")),
    )
    out_specs = (
        P(("grp", "slab"), None),
        P(("grp", "shot"), "slab", None),
        P(("grp", "shot"), "slab", None),
    )
    return jax.shard_map(local, mesh=mesh, in_specs=in_specs, out_specs=out_specs, check_vma=False)
```

time: 342 us -> 98.5 us (0.29)
  waiting for transfers between devices: 105 us -> 0 us
  Pallas kernels: 0 us -> 93.9 us
  starting transfers between devices: 72.9 us -> 0 us
  other arithmetic: 65.4 us -> 0 us
  matrix products: 50.3 us -> 0 us
  local copies, waits for them, and re-layouts: 31.5 us -> 3.76 us
  between operations: 14.3 us -> 0.65 us
    pallas_call x0 -> x1, Pallas kernels: none -> 93.9 us  [local(): pl.pallas_call(functools.partial(kernel, steps), name='rtm_window', out_s...]
    all_gather x1 -> x0, waiting for transfers between devices: 81.7 us -> none  [gathered_total(): blocks = lax.all_gather(shard, axis)]
    ppermute x18 -> x0, starting transfers between devices: 72.8 us -> none  [the longest x9 61.1 us: extended_2(): lax.ppermute(tail, axis, [(i, (i + 1) % count) for i in range(ends)])]
    dot_general x16 -> x0, matrix products: 50.3 us -> none  [advance(): jnp.einsum('szr,srx->szx', depth_table, lateral_table, precision=lax.Prec...]
    add x40 -> x0, other arithmetic: 41.2 us -> none  [the longest x16 39.8 us: laplace(): result + stencil_coeffs[offset] * (extended[..., 4 + offset:4 + offset +...]
    ppermute x18 -> x0, waiting for transfers between devices: 22.9 us -> none  [the longest x9 13.5 us: extended_2(): lax.ppermute(head, axis, [((i + 1) % count, i) for i in range(ends)])]
    while x160 -> x0, local copies, waits for them, and re-layouts: 18.2 us -> none
    gather x16 -> x0, local copies, waits for them, and re-layouts: 10.2 us -> none  [advance(): pulse = wavelet[checkpoint_step + STEPS - 1 - step_index]]
  transfers between devices with their start and end apart: 19 -> 0, of which waited for: 16 -> 0; matrix products, arithmetic and copies ran while one was open for 4% -> 0% of each run, Pallas kernels for 0% -> 0%
where the time goes in v1:
time: 98.5 us; the launch traced here: 98.3 us
  Pallas kernels  93.9 us (95%)
  local copies, waits for them, and re-layouts  3.76 us (4%)
    pallas_call x1, Pallas kernels, local(): pl.pallas_call(functools.partial(kernel, steps), name='rtm_window', out_s...  93.9 us
    unnamed x7, local copies, waits for them, and re-layouts  3.76 us

profile of v1, /device:TPU:65, one launch (start us, length us, event | category | flops | bytes accessed | tf_op | source)
XLA Modules:
  0.0 98.3 jit_solution(6705520432162800121)
XLA Ops:
  0.6 93.9 %rtm_window.1 = (f32[64,1024]{1,0:T(8,128)}, f32[2,64,1024]{2,1,0:T(8,128)}, f32[2,64,1024]{2,1,0:T(8,128)}) custom-call(f32[64,1024]{1,0:T(8,128)} %courant.1, s32[64,1024]{1,0:T(8,128)} %sponge.1, f32[2,64,1024]{2,1,0:T(8,128)} %src_hi.1, f32[2,64,1024]{2,1,0:T(8,128)} %src_now.1, f32[2,64,1024]{2,1,0:T(8,128)} %rec_hi.1, f32[2,64,1024]{2,1,0:T(8,128)} %rec_now.1, ...), custom_call_target="tpu_custom_call" | custom-call | tf_op jit(solution)/shard_map/rtm_window/pallas_call | solution.py:562
  94.5 0.0 copy-start.1
  94.5 1.7 %copy.19 = f32[64,1024]{1,0:T(8,128)} copy(f32[64,1024]{1,0:T(8,128)} %get-tuple-element.6) | data formatting | bytes 524288
  96.3 0.0 copy-done.1
  96.3 0.0 copy-start
  96.3 0.8 copy.20
  97.1 0.4 copy-done
  97.5 0.8 copy.21
Async XLA Ops:
  94.5 1.7 %copy-start.1 = (f32[2,64,1024]{2,1,0:T(8,128)S(1)}, f32[2,64,1024]{2,1,0:T(8,128)}, u32[]{:S(2)}) copy-start(f32[2,64,1024]{2,1,0:T(8,128)} %get-tuple-element.7) | copy-start | bytes 1572868
  96.3 1.2 %copy-start = (f32[2,64,1024]{2,1,0:T(8,128)S(1)}, f32[2,64,1024]{2,1,0:T(8,128)}, u32[]{:S(2)}) copy-start(f32[2,64,1024]{2,1,0:T(8,128)} %get-tuple-element.8) | copy-start | bytes 1572868

commit v2 on v1

--- a/solution.py
+++ b/solution.py
@@ -11,6 +11,7 @@
 MESH = pl.DeviceIdType.MESH
 F32 = jnp.float32
 BF16 = jnp.bfloat16
+VMEM_LIMIT = 48 * 1024 * 1024
 
 C0, C1, C2, C3, C4 = (-205.0 / 72.0, 8.0 / 5.0, -1.0 / 5.0, 8.0 / 315.0, -1.0 / 560.0)
 
@@ -23,55 +24,63 @@
 
 def kernel(
     steps,
-    courant,
-    sponge,
-    src_hi,
-    src_now,
-    rec_hi,
-    rec_now,
-    traces,
-    rec_depth,
-    rec_lateral,
-    wavelet,
-    src_depth,
-    src_lateral,
-    start_step,
-    image_out,
-    src_out,
-    rec_out,
-    N,
-    M,
-    V,
-    D,
-    AS,
-    VS,
-    AR,
-    VR,
-    G,
-    IA,
-    IB,
-    W,
-    DP,
-    T,
-    CORR,
-    PAIR,
-    HALF,
-    PARTS,
-    FIN,
-    IMG,
-    n_send,
-    n_recv,
-    h_send,
-    h_recv,
-    c_send,
-    c_recv,
-    pair_send,
-    pair_recv,
-    rs_send,
-    rs_recv,
-    ag_send,
-    ag_recv,
+    *refs,
 ):
+    inputs, refs = refs[:13], refs[13:]
+    (
+        image_out,
+        src_out,
+        rec_out,
+        courant,
+        sponge,
+        src_hi,
+        src_now,
+        rec_hi,
+        rec_now,
+        traces,
+        rec_depth,
+        rec_lateral,
+        wavelet,
+        src_depth,
+        src_lateral,
+        start_step,
+        R,
+        RV,
+        RS,
+        in_sem,
+        N,
+        M,
+        V,
+        D,
+        AS,
+        VS,
+        AR,
+        VR,
+        G,
+        IA,
+        IB,
+        W,
+        DP,
+        T,
+        CORR,
+        PAIR,
+        HALF,
+        PARTS,
+        FIN,
+        IMG,
+        n_send,
+        n_recv,
+        h_send,
+        h_recv,
+        c_send,
+        c_recv,
+        pair_send,
+        pair_recv,
+        rs_send,
+        rs_recv,
+        ag_send,
+        ag_recv,
+    ) = refs
     slab, slabs = lax.axis_index("slab"), lax.axis_size("slab")
     me, members = lax.axis_index("shot"), lax.axis_size("shot")
     chips = members // 2
@@ -105,6 +114,17 @@
     for peer in peers:
         greet({"shot": peer})
 
+    local_refs = (
+        courant, sponge, src_hi, src_now, rec_hi, rec_now, traces, rec_depth, rec_lateral,
+        wavelet, src_depth, src_lateral, start_step,
+    )
+    loads = [
+        pltpu.make_async_copy(inputs[i], local_refs[i], in_sem.at[i])
+        for i in (3, 2, 5, 4, 0, 1, 6, 7, 8, 9, 10, 11, 12)
+    ]
+    for load in loads:
+        load.start()
+
     lane = lax.broadcasted_iota(jnp.int32, (4, 8, 128), 2)
     lane8 = lax.broadcasted_iota(jnp.int32, (8, 8, 128), 2)
     reg8 = lax.broadcasted_iota(jnp.int32, (8, 8, 128), 0)
@@ -117,11 +137,11 @@
     def down_lane(v):
         return jnp.where(lane == 127, 0.0, pltpu.roll(v, 127, axis=2))
 
-    def to_registers(block, slot, put):
+    def to_registers(block, count, slot, put):
         for t in range(8):
-            T[slot, 128 * t : 128 * (t + 1), :] = block(t).T
+            T[slot, 128 * t : 128 * (t + 1), 0:count] = block(t).T
         for r in range(8):
-            put(r, T[slot, pl.ds(r, 128, stride=8), :].T)
+            put(r, T[slot, pl.ds(r, 128, stride=8), 0:count].T)
 
     def field_block(ref):
         return lambda t: ref[:, :, 128 * t : 128 * (t + 1)].reshape(shots * depth, 128)
@@ -162,27 +182,21 @@
 
     zeros = jnp.zeros((8, 8, 128), F32)
 
-    def clear(now_row, row):
+    def clear(side):
         for p in range(planes):
+            R[p, 16 * side : 16 * (side + 1), :] = jnp.zeros((16, 1024), F32)
             for slot in range(2):
-                N[slot, p, OWN, rows(now_row), :] = zeros
-            M[p, OWN, rows(row), :] = zeros
-        for ref in (V, D):
-            ref[:, rows(row), :] = zeros
+                N[slot, p, OWN, rows((8 + depth) * side), :] = zeros
+        RV[8 * side : 8 * (side + 1), :] = jnp.zeros((8, 1024), F32)
+        RS[8 * side : 8 * (side + 1), :] = jnp.zeros((8, 1024), jnp.int32)
 
     @pl.when(slab == 0)
     def _():
-        clear(0, 0)
+        clear(0)
 
     @pl.when(slab == slabs - 1)
     def _():
-        clear(8 + depth, depth)
-
-    to_registers(field_block(src_now), 0, put_now(0))
-    to_registers(field_block(src_hi), 1, put_hi(0))
-    to_registers(field_block(rec_now), 0, put_now(1))
-    to_registers(field_block(rec_hi), 1, put_hi(1))
-    to_registers(model_block, 0, put_model)
+        clear(1)
 
     def shift(ref_at, src_row, dst_row, count, send, recv, to):
         return pltpu.make_async_remote_copy(
@@ -200,19 +214,47 @@
             return shift(at, 8, 8 + depth, 8, n_send.at[p, 0], n_recv.at[slot, p, 0], slab - 1)
         return shift(at, depth, 0, 8, n_send.at[p, 1], n_recv.at[slot, p, 1], slab + 1)
 
-    def hi_copy(p, direction):
-        at = lambda row, count: M.at[p, OWN, pl.ds(row, count), :]
-        if direction == 0:
-            return shift(at, 4, 4 + depth, 4, h_send.at[p, 0], h_recv.at[p, 0], slab - 1)
-        return shift(at, depth, 0, 4, h_send.at[p, 1], h_recv.at[p, 1], slab + 1)
-
-    def model_copy(which, direction):
-        ref = (V, D)[which]
-        at = lambda row, count: ref.at[:, pl.ds(row, count), :]
-        sems = c_send.at[which, direction], c_recv.at[which, direction]
-        if direction == 0:
-            return shift(at, 4, 4 + depth, 4, *sems, slab - 1)
-        return shift(at, depth, 0, 4, *sems, slab + 1)
+    fields = (src_now, src_hi), (rec_now, rec_hi)
+
+    def raw(src, dst, send, recv, direction):
+        return pltpu.make_async_remote_copy(
+            src_ref=src,
+            dst_ref=dst,
+            send_sem=send,
+            recv_sem=recv,
+            device_id={"slab": slab - 1 if direction == 0 else slab + 1},
+            device_id_type=MESH,
+        )
+
+    def raw_now(p, direction):
+        row = 0 if direction == 0 else depth - 8
+        return raw(
+            fields[p % 2][0].at[p // 2, pl.ds(row, 8), :],
+            R.at[p, pl.ds(16 * (1 - direction), 8), :],
+            n_send.at[p, direction],
+            n_recv.at[0, p, direction],
+            direction,
+        )
+
+    def raw_hi(p, direction):
+        row = 0 if direction == 0 else depth - 4
+        return raw(
+            fields[p % 2][1].at[p // 2, pl.ds(row, 4), :],
+            R.at[p, pl.ds(16 * (1 - direction) + 8, 4), :],
+            h_send.at[p, direction],
+            h_recv.at[p, direction],
+            direction,
+        )
+
+    def raw_model(which, direction):
+        row = 0 if direction == 0 else depth - 4
+        return raw(
+            (courant, sponge)[which].at[pl.ds(row, 4), :],
+            (RV, RS)[which].at[pl.ds(8 * (1 - direction), 4), :],
+            c_send.at[which, direction],
+            c_recv.at[which, direction],
+            direction,
+        )
 
     def each_way(act):
         @pl.when(has_up)
@@ -228,14 +270,24 @@
     )
     pl.semaphore_wait(barrier, greeted)
 
+    for load in loads[:6]:
+        load.wait()
+
     def send_first(out, _):
-        model_copy(0, out).start()
-        model_copy(1, out).start()
+        raw_model(0, out).start()
+        raw_model(1, out).start()
         for p in range(planes):
-            hi_copy(p, out).start()
-            now_copy(0, p, out).start()
+            raw_now(p, out).start()
+            raw_hi(p, out).start()
 
     each_way(send_first)
+
+    to_registers(model_block, shots * depth, 0, put_model)
+    for field in range(2):
+        to_registers(field_block(fields[field][0]), shots * depth, 1, put_now(field))
+        to_registers(field_block(fields[field][1]), shots * depth, 0, put_hi(field))
+    for load in loads[6:]:
+        load.wait()
 
     pad = 16 * ((wide + 15) // 16)
     top = 2 * pad
@@ -253,6 +305,8 @@
                     (wanted == at + float(r)).astype(F32).astype(BF16)
                 )
 
+    span = 2 * (pad + depth)
+
     def inject(s, block):
         def terms(step):
             t = traces[s, pl.ds(step, 1), :] * (1.0 / C1)
@@ -261,20 +315,23 @@
 
         gap = jnp.zeros((pad - wide, nrec), F32)
         table = []
-        for term in terms(2 * block):
-            table += [DP[s] * term, gap]
-        for term in terms(2 * block + 1):
-            table += [DP[s, 4 : 4 + depth, :] * term]
+        for e in range(2):
+            for term in terms(2 * (block + e)):
+                table += [DP[s] * term, gap]
+            for term in terms(2 * (block + e) + 1):
+                table += [DP[s, 4 : 4 + depth, :] * term]
         table = jnp.concatenate(table, axis=0).astype(BF16)
         for c in range(4):
-            got = jnp.dot(
+            both = jnp.dot(
                 table, W[s, :, 256 * c : 256 * (c + 1)], preferred_element_type=F32
             )
-            a = got[0:wide] + got[pad : pad + wide]
-            b = got[top : top + depth] + got[top + depth : top + 2 * depth]
             for e in range(2):
-                IA[s, 2 * c + e] = a[:, 128 * e : 128 * (e + 1)]
-                IB[s, 2 * c + e] = b[:, 128 * e : 128 * (e + 1)]
+                got = both[span * e : span * (e + 1)]
+                a = got[0:wide] + got[pad : pad + wide]
+                b = got[top : top + depth] + got[top + depth : top + 2 * depth]
+                for h in range(2):
+                    IA[s, block + e, 2 * c + h] = a[:, 128 * h : 128 * (h + 1)]
+                    IB[s, block + e, 2 * c + h] = b[:, 128 * h : 128 * (h + 1)]
 
     def coefficients(m):
         at = rows(m)
@@ -316,17 +373,17 @@
         ref[pre + (slice(12, 16), at, slice(None))] = down_lane(value[:4])
         ref[pre + (slice(0, 4), at, slice(None))] = up_lane(value[4:])
 
-    def first_step(slot, s, field, g, pulse, stored):
+    def first_step(slot, b, s, field, g, pulse, stored):
         p, m = 2 * s + field, 8 * g
         X, z = neighbours(N, (slot, p), m + 4, stored)
-        injected = IA[s, :, rows(m), :] if field else None
+        injected = IA[s, b, :, rows(m), :] if field else None
         new = advance(field, s, z(0), spread(X, z), M[p, OWN, rows(m), :], m, injected, pulse)
         put_field(M, (p,), m, new)
 
-    def second_step(slot, to, s, field, g, pulse, final=False):
+    def second_step(slot, to, b, s, field, g, pulse, final=False):
         p, m = 2 * s + field, 8 * g + 4
         X, z = neighbours(M, (p,), m, True)
-        injected = IB[s, :, rows(8 * g), :] if field else None
+        injected = IB[s, b, :, rows(8 * g), :] if field else None
         hi = N[slot, p, OWN, rows(8 * g + 8), :]
         centre = z(0)
         new = advance(field, s, centre, spread(X, z), hi, m, injected, pulse)
@@ -354,19 +411,14 @@
         for field in range(2):
             pulse = pulse_of(s, 0)
             for g in range(1, groups):
-                first_step(0, s, field, g, pulse, True)
-
-    def arrive_first(out, inn):
-        for which in range(2):
-            model_copy(which, out).wait_send()
-            model_copy(which, inn).wait_recv()
-
-    def arrive_hi(p):
-        def act(out, inn):
-            hi_copy(p, out).wait_send()
-            hi_copy(p, inn).wait_recv()
-
-        return act
+                first_step(0, 0, s, field, g, pulse, True)
+
+    def later_blocks(i, carry):
+        for s in range(shots):
+            inject(s, 2 * i)
+        return carry
+
+    lax.fori_loop(1, blocks // 2, later_blocks, 0)
 
     def arrive_now(slot, p):
         def act(out, inn):
@@ -381,35 +433,82 @@
 
         return act
 
-    each_way(arrive_first)
+    def arrive_raw(copies):
+        def act(out, inn):
+            for copy in copies:
+                copy(out).wait_send()
+                copy(inn).wait_recv()
+
+        return act
+
+    each_way(arrive_raw([functools.partial(raw_model, 0), functools.partial(raw_model, 1)]))
+
+    def edge_model(t):
+        cols = slice(128 * t, 128 * (t + 1))
+        return jnp.concatenate([RV[:, cols], 1.0 - 0.06 * RS[:, cols].astype(F32)], axis=0)
+
+    def put_edge_model(r, value):
+        V[r, 0:4, :] = value[0:4]
+        V[r, 4 + depth : 8 + depth, :] = value[8:12]
+        D[r, 0:4, :] = value[16:20]
+        D[r, 4 + depth : 8 + depth, :] = value[24:28]
+
+    to_registers(edge_model, 32, 0, put_edge_model)
     coefficients(0)
     coefficients(8 * groups)
+
+    def edge_rows(p):
+        def put(r, value):
+            N[0, p, 4 + r, 0:8, :] = value[0:8]
+            M[p, 4 + r, 0:4, :] = value[8:12]
+            N[0, p, 4 + r, 8 + depth : 16 + depth, :] = value[16:24]
+            M[p, 4 + r, 4 + depth : 8 + depth, :] = value[24:28]
+
+        to_registers(lambda t: R[p, :, 128 * t : 128 * (t + 1)], 32, (p + 1) % 2, put)
+
     for p in range(planes):
-        each_way(arrive_hi(p))
+        each_way(arrive_raw([functools.partial(raw_now, p), functools.partial(raw_hi, p)]))
+        edge_rows(p)
+        for g in (0, groups):
+            first_step(0, 0, p // 2, p % 2, g, pulse_of(p // 2, 0), False)
+        for g in (0, groups - 1):
+            second_step(0, 1, 0, p // 2, p % 2, g, pulse_of(p // 2, 1))
+        each_way(send_now(1, p))
+
+    def edges(b, slot, to, s, field, pulses):
+        p = 2 * s + field
+        each_way(arrive_now(slot, p))
+        for g in (0, groups):
+            first_step(slot, b, s, field, g, pulses[0], False)
+        for g in (0, groups - 1):
+            second_step(slot, to, b, s, field, g, pulses[1])
+        each_way(send_now(to, p))
+
+    def inner(b, slot, to, s, pulses):
+        for field in range(2):
+            for g in range(1, groups - 1):
+                second_step(slot, to, b, s, field, g, pulses[1])
+        for field in range(2):
+            for g in range(1, groups):
+                first_step(to, b + 1, s, field, g, pulses[2], True)
+
+    def pulses_of(s, b):
+        return [pulse_of(s, 2 * b + j) for j in range(3)]
+
+    for s in range(shots):
+        inner(0, 0, 1, s, pulses_of(s, 0))
 
     def block(b, carry):
         slot = lax.rem(b, 2)
         to = 1 - slot
         for s in range(shots):
-            pulses = [pulse_of(s, 2 * b + j) for j in range(3)]
+            pulses = pulses_of(s, b)
             for field in range(2):
-                p = 2 * s + field
-                each_way(arrive_now(slot, p))
-                for g in (0, groups):
-                    first_step(slot, s, field, g, pulses[0], False)
-                for g in (0, groups - 1):
-                    second_step(slot, to, s, field, g, pulses[1])
-                each_way(send_now(to, p))
-            for field in range(2):
-                for g in range(1, groups - 1):
-                    second_step(slot, to, s, field, g, pulses[1])
-            inject(s, b + 1)
-            for field in range(2):
-                for g in range(1, groups):
-                    first_step(to, s, field, g, pulses[2], True)
+                edges(b, slot, to, s, field, pulses)
+            inner(b, slot, to, s, pulses)
         return carry
 
-    lax.fori_loop(0, blocks - 1, block, 0)
+    lax.fori_loop(1, blocks - 1, block, 0)
 
     last = blocks - 1
     slot = last % 2
@@ -419,7 +518,7 @@
             p = 2 * s + field
             each_way(arrive_now(slot, p))
             for g in (0, groups):
-                first_step(slot, s, field, g, pulse_of(s, 2 * last), False)
+                first_step(slot, last, s, field, g, pulse_of(s, 2 * last), False)
     for g in range(groups):
         total = CORR[:, rows(8 * g), :]
         for s in range(shots):
@@ -445,7 +544,7 @@
     for s in range(shots):
         for field in range(2):
             for g in range(groups // 2):
-                second_step(slot, to, s, field, g, pulse_of(s, steps - 1), True)
+                second_step(slot, to, last, s, field, g, pulse_of(s, steps - 1), True)
     pair.wait()
     HALF[...] = CORR[mine] + PAIR[...]
 
@@ -468,7 +567,7 @@
     for s in range(shots):
         for field in range(2):
             for g in range(groups // 2, groups):
-                second_step(slot, to, s, field, g, pulse_of(s, steps - 1), True)
+                second_step(slot, to, last, s, field, g, pulse_of(s, steps - 1), True)
 
     def from_registers(get, count, slot, put):
         for r in range(8):
@@ -529,10 +628,25 @@
         gather(d).wait_send()
     swap.wait()
 
-    def image_put(t, value):
-        image_out[:, 128 * t : 128 * (t + 1)] = value
-
-    from_registers(lambda r: IMG[r], depth, 0, image_put)
+    image_out[...] = IMG[...]
+
+
+def finish(image, src, rec, image_out, src_out, rec_out, T, natural, sem):
+    copies = [
+        pltpu.make_async_copy(src, src_out, sem.at[1]),
+        pltpu.make_async_copy(rec, rec_out, sem.at[2]),
+    ]
+    for copy in copies:
+        copy.start()
+    depth = image.shape[1]
+    for r in range(8):
+        T[pl.ds(r, 128, stride=8), 0:depth] = image[r].T
+    for t in range(8):
+        natural[:, 128 * t : 128 * (t + 1)] = T[128 * t : 128 * (t + 1), 0:depth].T
+    copies.append(pltpu.make_async_copy(natural, image_out, sem.at[0]))
+    copies[-1].start()
+    for copy in copies:
+        copy.wait()
 
 
 def local(
@@ -558,24 +672,37 @@
     wide = depth + 8
     planes = 2 * shots
     vmem = pl.BlockSpec(memory_space=pltpu.VMEM)
-    smem = pl.BlockSpec(memory_space=pltpu.SMEM)
-    return pl.pallas_call(
+    image, src_out, rec_out = pl.pallas_call(
         functools.partial(kernel, steps),
         name="rtm_window",
         out_shape=(
-            jax.ShapeDtypeStruct((depth, lateral), F32),
+            jax.ShapeDtypeStruct((8, depth, 128), F32),
             jax.ShapeDtypeStruct((shots, depth, lateral), F32),
             jax.ShapeDtypeStruct((shots, depth, lateral), F32),
         ),
-        in_specs=[vmem] * 9 + [smem] * 4,
+        in_specs=[pl.BlockSpec(memory_space=pltpu.HBM)] * 13,
         out_specs=(vmem, vmem, vmem),
         scratch_shapes=[
+            pltpu.VMEM((depth, lateral), F32),
+            pltpu.VMEM((depth, lateral), jnp.int32),
+            *[pltpu.VMEM((shots, depth, lateral), F32) for _ in range(4)],
+            pltpu.VMEM(traces.shape, F32),
+            pltpu.VMEM(receiver_depth.shape, jnp.int32),
+            pltpu.VMEM(receiver_lateral.shape, jnp.int32),
+            pltpu.SMEM(wavelet.shape, F32),
+            pltpu.SMEM(source_depth.shape, jnp.int32),
+            pltpu.SMEM(source_lateral.shape, jnp.int32),
+            pltpu.SMEM(checkpoint_step.shape, jnp.int32),
+            pltpu.VMEM((planes, 32, lateral), F32),
+            pltpu.VMEM((16, lateral), F32),
+            pltpu.VMEM((16, lateral), jnp.int32),
+            pltpu.SemaphoreType.DMA((13,)),
             pltpu.VMEM((2, planes, 16, depth + 16, 128), F32),
             pltpu.VMEM((planes, 16, wide, 128), F32),
             *[pltpu.VMEM((8, wide, 128), F32) for _ in range(6)],
             pltpu.VMEM((shots, 8, wide, 128), F32),
-            pltpu.VMEM((shots, 8, wide, 128), F32),
-            pltpu.VMEM((shots, 8, depth, 128), F32),
+            pltpu.VMEM((shots, steps // 2, 8, wide, 128), F32),
+            pltpu.VMEM((shots, steps // 2, 8, depth, 128), F32),
             pltpu.VMEM((shots, nrec, lateral), BF16),
             pltpu.VMEM((shots, wide, nrec), F32),
             pltpu.VMEM((2, lateral, 128), F32),
@@ -598,22 +725,46 @@
             pltpu.SemaphoreType.DMA((chips,)),
             pltpu.SemaphoreType.DMA((chips,)),
         ],
-        compiler_params=pltpu.CompilerParams(collective_id=0, has_side_effects=True),
+        compiler_params=pltpu.CompilerParams(
+            collective_id=0, has_side_effects=True, vmem_limit_bytes=VMEM_LIMIT
+        ),
     )(
-        courant_sq,
-        sponge_level,
-        source_later,
-        source_now,
-        receiver_later,
-        receiver_now,
-        traces,
-        receiver_depth,
-        receiver_lateral,
-        wavelet,
-        source_depth,
-        source_lateral,
-        checkpoint_step,
+        *[
+            pltpu.with_memory_space_constraint(x, pltpu.HBM)
+            for x in (
+                courant_sq,
+                sponge_level,
+                source_later,
+                source_now,
+                receiver_later,
+                receiver_now,
+                traces,
+                receiver_depth,
+                receiver_lateral,
+                wavelet,
+                source_depth,
+                source_lateral,
+                checkpoint_step,
+            )
+        ]
     )
+    return pl.pallas_call(
+        finish,
+        name="finish",
+        out_shape=(
+            jax.ShapeDtypeStruct((depth, lateral), F32),
+            jax.ShapeDtypeStruct((shots, depth, lateral), F32),
+            jax.ShapeDtypeStruct((shots, depth, lateral), F32),
+        ),
+        in_specs=[vmem] * 3,
+        out_specs=(pl.BlockSpec(memory_space=pltpu.HBM),) * 3,
+        scratch_shapes=[
+            pltpu.VMEM((lateral, 128), F32),
+            pltpu.VMEM((depth, lateral), F32),
+            pltpu.SemaphoreType.DMA((3,)),
+        ],
+        compiler_params=pltpu.CompilerParams(vmem_limit_bytes=VMEM_LIMIT),
+    )(image, src_out, rec_out)
 
 
 def solution(mesh):

time: 98.5 us -> 97.3 us (0.988)
  local copies, waits for them, and re-layouts: 3.76 us -> 0 us
  Pallas kernels: 93.9 us -> 96.3 us
    unnamed x7 -> x0, local copies, waits for them, and re-layouts: 3.76 us -> none
    pallas_call x1, Pallas kernels: 93.9 us -> 95.2 us  [local(): pl.pallas_call(functools.partial(kernel, steps), name='rtm_window', out_s...]
    pallas_call x0 -> x1, Pallas kernels: none -> 1.1 us  [local(): pl.pallas_call(finish, name='finish', out_shape=(jax.ShapeDtypeStruct((de...]
where the time goes in v2:
time: 97.3 us; the launch traced here: 97.1 us
  Pallas kernels  96.3 us (99%)
    pallas_call x1, Pallas kernels, local(): pl.pallas_call(functools.partial(kernel, steps), name='rtm_window', out_s...  95.2 us

profile of v2, /device:TPU:65, one launch (start us, length us, event | category | flops | bytes accessed | tf_op | source)
XLA Modules:
  0.0 97.1 jit_solution(13467032800905281795)
XLA Ops:
  0.6 95.2 %rtm_window.1 = (f32[8,64,128]{2,1,0:T(8,128)S(1)}, f32[2,64,1024]{2,1,0:T(8,128)S(1)}, f32[2,64,1024]{2,1,0:T(8,128)S(1)}) custom-call(f32[64,1024]{1,0:T(8,128)} %refs_0_.1, s32[64,1024]{1,0:T(8,128)} %refs_1_.1, f32[2,64,1024]{2,1,0:T(8,128)} %refs_2_.1, f32[2,64,1024]{2,1,0:T(8,128)} %refs_3_.1, f32[2,64,1024]{2,1,0:T(8,128)} %refs_4_.1, ...), custom_call_target="tpu_custom_call" | custom-call | tf_op jit(solution)/shard_map/rtm_window/pallas_call | solution.py:675
  95.9 1.1 %finish.1 = (f32[64,1024]{1,0:T(8,128)}, f32[2,64,1024]{2,1,0:T(8,128)}, f32[2,64,1024]{2,1,0:T(8,128)}) custom-call(f32[8,64,128]{2,1,0:T(8,128)S(1)} %get-tuple-element.6.image, f32[2,64,1024]{2,1,0:T(8,128)S(1)} %get-tuple-element.7.src, f32[2,64,1024]{2,1,0:T(8,128)S(1)} %get-tuple-element.8.rec), custom_call_target="tpu_custom_call" | custom-call | tf_op jit(solution)/shard_map/finish/pallas_call | solution.py:751

commit v3 on v2

--- a/solution.py
+++ b/solution.py
@@ -68,6 +68,11 @@
         PARTS,
         FIN,
         IMG,
+        LATE,
+        LPAIR,
+        LHALF,
+        LPARTS,
+        LSUM,
         n_send,
         n_recv,
         h_send,
@@ -80,6 +85,8 @@
         rs_recv,
         ag_send,
         ag_recv,
+        l_send,
+        l_recv,
     ) = refs
     slab, slabs = lax.axis_index("slab"), lax.axis_size("slab")
     me, members = lax.axis_index("shot"), lax.axis_size("shot")
@@ -120,7 +127,7 @@
     )
     loads = [
         pltpu.make_async_copy(inputs[i], local_refs[i], in_sem.at[i])
-        for i in (3, 2, 5, 4, 0, 1, 6, 7, 8, 9, 10, 11, 12)
+        for i in (0, 1, 3, 2, 5, 4, 9, 10, 11, 12, 6, 7, 8)
     ]
     for load in loads:
         load.start()
@@ -276,34 +283,38 @@
     def send_first(out, _):
         raw_model(0, out).start()
         raw_model(1, out).start()
-        for p in range(planes):
-            raw_now(p, out).start()
-            raw_hi(p, out).start()
+        for field in range(2):
+            for s in range(shots):
+                raw_now(2 * s + field, out).start()
+                raw_hi(2 * s + field, out).start()
 
     each_way(send_first)
 
-    to_registers(model_block, shots * depth, 0, put_model)
-    for field in range(2):
+    def field_in(field):
         to_registers(field_block(fields[field][0]), shots * depth, 1, put_now(field))
         to_registers(field_block(fields[field][1]), shots * depth, 0, put_hi(field))
+
+    to_registers(model_block, shots * depth, 0, put_model)
+    field_in(0)
     for load in loads[6:]:
         load.wait()
 
     pad = 16 * ((wide + 15) // 16)
     top = 2 * pad
 
-    rec_ids = first - 4 + lax.broadcasted_iota(jnp.int32, (wide, nrec), 0)
-    for s in range(shots):
-        DP[s] = (rec_ids == rec_depth[s : s + 1, :]).astype(F32)
-        for q in range(nrec // 128):
-            wanted = jnp.broadcast_to(
-                rec_lateral[s : s + 1, 128 * q : 128 * (q + 1)].astype(F32), (128, 128)
-            ).T
-            at = lax.broadcasted_iota(jnp.int32, (128, 128), 1).astype(F32) * 8.0
-            for r in range(8):
-                W[s, 128 * q : 128 * (q + 1), 128 * r : 128 * (r + 1)] = (
-                    (wanted == at + float(r)).astype(F32).astype(BF16)
-                )
+    def tables():
+        rec_ids = first - 4 + lax.broadcasted_iota(jnp.int32, (wide, nrec), 0)
+        for s in range(shots):
+            DP[s] = (rec_ids == rec_depth[s : s + 1, :]).astype(F32)
+            for q in range(nrec // 128):
+                wanted = jnp.broadcast_to(
+                    rec_lateral[s : s + 1, 128 * q : 128 * (q + 1)].astype(F32), (128, 128)
+                ).T
+                at = lax.broadcasted_iota(jnp.int32, (128, 128), 1).astype(F32) * 8.0
+                for r in range(8):
+                    W[s, 128 * q : 128 * (q + 1), 128 * r : 128 * (r + 1)] = (
+                        (wanted == at + float(r)).astype(F32).astype(BF16)
+                    )
 
     span = 2 * (pad + depth)
 
@@ -402,24 +413,6 @@
     def pulse_of(s, step):
         return wavelet[start_step[s] + steps - 1 - step]
 
-    for g in range(1, groups):
-        coefficients(8 * g)
-    for g in range(groups):
-        CORR[:, rows(8 * g), :] = zeros
-    for s in range(shots):
-        inject(s, 0)
-        for field in range(2):
-            pulse = pulse_of(s, 0)
-            for g in range(1, groups):
-                first_step(0, 0, s, field, g, pulse, True)
-
-    def later_blocks(i, carry):
-        for s in range(shots):
-            inject(s, 2 * i)
-        return carry
-
-    lax.fori_loop(1, blocks // 2, later_blocks, 0)
-
     def arrive_now(slot, p):
         def act(out, inn):
             now_copy(slot, p, out).wait_send()
@@ -441,8 +434,6 @@
 
         return act
 
-    each_way(arrive_raw([functools.partial(raw_model, 0), functools.partial(raw_model, 1)]))
-
     def edge_model(t):
         cols = slice(128 * t, 128 * (t + 1))
         return jnp.concatenate([RV[:, cols], 1.0 - 0.06 * RS[:, cols].astype(F32)], axis=0)
@@ -453,27 +444,55 @@
         D[r, 0:4, :] = value[16:20]
         D[r, 4 + depth : 8 + depth, :] = value[24:28]
 
+    def edge_rows(field):
+        def block(t):
+            cols = slice(128 * t, 128 * (t + 1))
+            return jnp.concatenate([R[2 * s + field, :, cols] for s in range(shots)], axis=0)
+
+        def put(r, value):
+            for s in range(shots):
+                p, at = 2 * s + field, 32 * s
+                N[0, p, 4 + r, 0:8, :] = value[at : at + 8]
+                M[p, 4 + r, 0:4, :] = value[at + 8 : at + 12]
+                N[0, p, 4 + r, 8 + depth : 16 + depth, :] = value[at + 16 : at + 24]
+                M[p, 4 + r, 4 + depth : 8 + depth, :] = value[at + 24 : at + 28]
+
+        to_registers(block, 32 * shots, 1, put)
+
+    for g in range(1, groups):
+        coefficients(8 * g)
+    for g in range(groups):
+        CORR[:, rows(8 * g), :] = zeros
+    each_way(arrive_raw([functools.partial(raw_model, 0), functools.partial(raw_model, 1)]))
     to_registers(edge_model, 32, 0, put_edge_model)
     coefficients(0)
     coefficients(8 * groups)
 
-    def edge_rows(p):
-        def put(r, value):
-            N[0, p, 4 + r, 0:8, :] = value[0:8]
-            M[p, 4 + r, 0:4, :] = value[8:12]
-            N[0, p, 4 + r, 8 + depth : 16 + depth, :] = value[16:24]
-            M[p, 4 + r, 4 + depth : 8 + depth, :] = value[24:28]
-
-        to_registers(lambda t: R[p, :, 128 * t : 128 * (t + 1)], 32, (p + 1) % 2, put)
-
-    for p in range(planes):
-        each_way(arrive_raw([functools.partial(raw_now, p), functools.partial(raw_hi, p)]))
-        edge_rows(p)
-        for g in (0, groups):
-            first_step(0, 0, p // 2, p % 2, g, pulse_of(p // 2, 0), False)
-        for g in (0, groups - 1):
-            second_step(0, 1, 0, p // 2, p % 2, g, pulse_of(p // 2, 1))
-        each_way(send_now(1, p))
+    def first_edges(field):
+        for s in range(shots):
+            for g in (1, groups - 1):
+                first_step(0, 0, s, field, g, pulse_of(s, 0), True)
+        for s in range(shots):
+            p = 2 * s + field
+            each_way(arrive_raw([functools.partial(raw_now, p), functools.partial(raw_hi, p)]))
+        edge_rows(field)
+        for s in range(shots):
+            for g in (0, groups):
+                first_step(0, 0, s, field, g, pulse_of(s, 0), False)
+            for g in (0, groups - 1):
+                second_step(0, 1, 0, s, field, g, pulse_of(s, 1))
+            each_way(send_now(1, 2 * s + field))
+
+    first_edges(0)
+    field_in(1)
+    tables()
+    for s in range(shots):
+        inject(s, 0)
+    first_edges(1)
+    for s in range(shots):
+        for field in range(2):
+            for g in range(2, groups - 1):
+                first_step(0, 0, s, field, g, pulse_of(s, 0), True)
 
     def edges(b, slot, to, s, field, pulses):
         p = 2 * s + field
@@ -484,10 +503,12 @@
             second_step(slot, to, b, s, field, g, pulses[1])
         each_way(send_now(to, p))
 
-    def inner(b, slot, to, s, pulses):
+    def inner(b, slot, to, s, pulses, products=False):
         for field in range(2):
             for g in range(1, groups - 1):
                 second_step(slot, to, b, s, field, g, pulses[1])
+        if products:
+            inject(s, b + 1)
         for field in range(2):
             for g in range(1, groups):
                 first_step(to, b + 1, s, field, g, pulses[2], True)
@@ -498,34 +519,32 @@
     for s in range(shots):
         inner(0, 0, 1, s, pulses_of(s, 0))
 
-    def block(b, carry):
-        slot = lax.rem(b, 2)
-        to = 1 - slot
-        for s in range(shots):
-            pulses = pulses_of(s, b)
-            for field in range(2):
-                edges(b, slot, to, s, field, pulses)
-            inner(b, slot, to, s, pulses)
+    def two_blocks(i, carry):
+        for e in range(2):
+            b, slot, to = 2 * i + 1 + e, 1 - e, e
+            for s in range(shots):
+                pulses = pulses_of(s, b)
+                for field in range(2):
+                    edges(b, slot, to, s, field, pulses)
+                inner(b, slot, to, s, pulses, e == 0)
         return carry
 
-    lax.fori_loop(1, blocks - 1, block, 0)
+    lax.fori_loop(0, blocks // 2 - 1, two_blocks, 0)
 
     last = blocks - 1
-    slot = last % 2
-    to = 1 - slot
-    for s in range(shots):
-        for field in range(2):
-            p = 2 * s + field
-            each_way(arrive_now(slot, p))
-            for g in (0, groups):
-                first_step(slot, last, s, field, g, pulse_of(s, 2 * last), False)
+    slot, to = 1, 0
     for g in range(groups):
         total = CORR[:, rows(8 * g), :]
         for s in range(shots):
             at = rows(8 * g + 8)
             total = total + N[slot, 2 * s, OWN, at, :] * N[slot, 2 * s + 1, OWN, at, :]
             at = rows(8 * g + 4)
-            total = total + M[2 * s, OWN, at, :] * M[2 * s + 1, OWN, at, :]
+            product = M[2 * s, OWN, at, :] * M[2 * s + 1, OWN, at, :]
+            if g == 0:
+                product = jnp.where(row8 < 4, 0.0, product)
+            if g == groups - 1:
+                product = jnp.where(row8 < 4, product, 0.0)
+            total = total + product
         CORR[:, rows(8 * g), :] = total
 
     def remote(src, dst, send, recv, shot):
@@ -541,10 +560,14 @@
     mine = pl.ds(4 * core, 4)
     pair = remote(CORR.at[pl.ds(4 * (1 - core), 4)], PAIR, pair_send.at[0], pair_recv.at[0], partner)
     pair.start()
-    for s in range(shots):
-        for field in range(2):
-            for g in range(groups // 2):
-                second_step(slot, to, last, s, field, g, pulse_of(s, steps - 1), True)
+
+    def final_step(wanted):
+        for s in range(shots):
+            for field in range(2):
+                for g in wanted:
+                    second_step(slot, to, last, s, field, g, pulse_of(s, steps - 1), True)
+
+    final_step(range(1, groups - 1))
     pair.wait()
     HALF[...] = CORR[mine] + PAIR[...]
 
@@ -564,10 +587,41 @@
     order = sorted(range(1, chips), key=lambda d: -min(d, chips - d))
     for d in order:
         scatter(d).start()
+
     for s in range(shots):
         for field in range(2):
-            for g in range(groups // 2, groups):
-                second_step(slot, to, last, s, field, g, pulse_of(s, steps - 1), True)
+            each_way(arrive_now(slot, 2 * s + field))
+            for g in (0, groups):
+                first_step(slot, last, s, field, g, pulse_of(s, 2 * last), False)
+
+    late = zeros
+    for s in range(shots):
+        low, high = rows(4), rows(depth - 4)
+        late = late + jnp.where(
+            row8 < 4,
+            M[2 * s, OWN, low, :] * M[2 * s + 1, OWN, low, :],
+            M[2 * s, OWN, high, :] * M[2 * s + 1, OWN, high, :],
+        )
+    LATE[...] = late
+    late_pair = remote(
+        LATE.at[pl.ds(4 * (1 - core), 4)], LPAIR, pair_send.at[2], pair_recv.at[2], partner
+    )
+    late_pair.start()
+    final_step((0, groups - 1))
+    late_pair.wait()
+    LHALF[...] = LATE[mine] + LPAIR[...]
+
+    def spread_late(d):
+        other = lax.rem(chip + d, chips)
+        return remote(
+            LHALF, LPARTS.at[chips - d], l_send.at[d], l_recv.at[chips - d], other * 2 + core
+        )
+
+    def late_from(d):
+        return remote(LHALF, LPARTS.at[d], l_send.at[d], l_recv.at[d], partner)
+
+    for d in order:
+        spread_late(d).start()
 
     def from_registers(get, count, slot, put):
         for r in range(8):
@@ -587,7 +641,6 @@
 
         from_registers(get, shots * depth, field, put)
 
-    field_out(0, src_out)
     for d in order:
         scattered(d).wait_recv()
     total = HALF[:, pl.ds(chip * part, part), :]
@@ -618,7 +671,16 @@
     for d in order:
         gather(d).start()
     IMG[mine, pl.ds(chip * part, part), :] = FIN[...]
+    field_out(0, src_out)
     field_out(1, rec_out)
+    for d in order:
+        late_from(d).wait_recv()
+    total = LHALF[...]
+    for d in range(1, chips):
+        total = total + LPARTS[d]
+    LSUM[mine] = total * (1.0 / math.sqrt(steps * shots * members))
+    late_swap = remote(LSUM.at[mine], LSUM.at[mine], pair_send.at[3], pair_recv.at[3], partner)
+    late_swap.start()
     for d in order:
         gathered(d).wait_recv()
     swap = remote(IMG.at[mine], IMG.at[mine], pair_send.at[1], pair_recv.at[1], partner)
@@ -626,9 +688,17 @@
     for d in range(1, chips):
         scatter(d).wait_send()
         gather(d).wait_send()
+        spread_late(d).wait_send()
+    late_swap.wait()
     swap.wait()
 
-    image_out[...] = IMG[...]
+    for g in range(groups):
+        value = IMG[:, rows(8 * g), :]
+        if g == 0:
+            value = value + jnp.where(row8 < 4, LSUM[...], 0.0)
+        if g == groups - 1:
+            value = value + jnp.where(row8 < 4, 0.0, LSUM[...])
+        image_out[:, rows(8 * g), :] = value
 
 
 def finish(image, src, rec, image_out, src_out, rec_out, T, natural, sem):
@@ -712,14 +782,21 @@
             pltpu.VMEM((chips, 4, part, 128), F32),
             pltpu.VMEM((4, part, 128), F32),
             pltpu.VMEM((8, depth, 128), F32),
+            pltpu.VMEM((8, 8, 128), F32),
+            pltpu.VMEM((4, 8, 128), F32),
+            pltpu.VMEM((4, 8, 128), F32),
+            pltpu.VMEM((chips, 4, 8, 128), F32),
+            pltpu.VMEM((8, 8, 128), F32),
             pltpu.SemaphoreType.DMA((planes, 2)),
             pltpu.SemaphoreType.DMA((2, planes, 2)),
             pltpu.SemaphoreType.DMA((planes, 2)),
             pltpu.SemaphoreType.DMA((planes, 2)),
             pltpu.SemaphoreType.DMA((2, 2)),
             pltpu.SemaphoreType.DMA((2, 2)),
-            pltpu.SemaphoreType.DMA((2,)),
-            pltpu.SemaphoreType.DMA((2,)),
+            pltpu.SemaphoreType.DMA((4,)),
+            pltpu.SemaphoreType.DMA((4,)),
+            pltpu.SemaphoreType.DMA((chips,)),
+            pltpu.SemaphoreType.DMA((chips,)),
             pltpu.SemaphoreType.DMA((chips,)),
             pltpu.SemaphoreType.DMA((chips,)),
             pltpu.SemaphoreType.DMA((chips,)),

time: 97.3 us -> 94.1 us (0.967)
  Pallas kernels: 96.3 us -> 93.1 us
    pallas_call x1, Pallas kernels: 95.2 us -> 92 us  [local(): pl.pallas_call(functools.partial(kernel, steps), name='rtm_window', out_s...]
where the time goes in v3:
time: 94.1 us; the launch traced here: 93.9 us
  Pallas kernels  93.1 us (99%)
    pallas_call x1, Pallas kernels, local(): pl.pallas_call(functools.partial(kernel, steps), name='rtm_window', out_s...  92 us

profile of v3, /device:TPU:65, one launch (start us, length us, event | category | flops | bytes accessed | tf_op | source)
XLA Modules:
  0.0 93.9 jit_solution(840416252434726900)
XLA Ops:
  0.6 92.0 %rtm_window.1 = (f32[8,64,128]{2,1,0:T(8,128)S(1)}, f32[2,64,1024]{2,1,0:T(8,128)S(1)}, f32[2,64,1024]{2,1,0:T(8,128)S(1)}) custom-call(f32[64,1024]{1,0:T(8,128)} %refs_0_.1, s32[64,1024]{1,0:T(8,128)} %refs_1_.1, f32[2,64,1024]{2,1,0:T(8,128)} %refs_2_.1, f32[2,64,1024]{2,1,0:T(8,128)} %refs_3_.1, f32[2,64,1024]{2,1,0:T(8,128)} %refs_4_.1, ...), custom_call_target="tpu_custom_call" | custom-call | tf_op jit(solution)/shard_map/rtm_window/pallas_call | solution.py:745
  92.7 1.1 %finish.1 = (f32[64,1024]{1,0:T(8,128)}, f32[2,64,1024]{2,1,0:T(8,128)}, f32[2,64,1024]{2,1,0:T(8,128)}) custom-call(f32[8,64,128]{2,1,0:T(8,128)S(1)} %get-tuple-element.6.image, f32[2,64,1024]{2,1,0:T(8,128)S(1)} %get-tuple-element.7.src, f32[2,64,1024]{2,1,0:T(8,128)S(1)} %get-tuple-element.8.rec), custom_call_target="tpu_custom_call" | custom-call | tf_op jit(solution)/shard_map/finish/pallas_call | solution.py:828

commit v4 on v3

--- a/solution.py
+++ b/solution.py
@@ -57,8 +57,10 @@
         AR,
         VR,
         G,
-        IA,
-        IB,
+        IA0,
+        IA1,
+        IB0,
+        IB1,
         W,
         DP,
         T,
@@ -88,6 +90,7 @@
         l_send,
         l_recv,
     ) = refs
+    IA, IB = (IA0, IA1), (IB0, IB1)
     slab, slabs = lax.axis_index("slab"), lax.axis_size("slab")
     me, members = lax.axis_index("shot"), lax.axis_size("shot")
     chips = members // 2
@@ -316,9 +319,7 @@
                         (wanted == at + float(r)).astype(F32).astype(BF16)
                     )
 
-    span = 2 * (pad + depth)
-
-    def inject(s, block):
+    def inject(s, parity, block):
         def terms(step):
             t = traces[s, pl.ds(step, 1), :] * (1.0 / C1)
             hi = t.astype(BF16).astype(F32)
@@ -326,23 +327,18 @@
 
         gap = jnp.zeros((pad - wide, nrec), F32)
         table = []
-        for e in range(2):
-            for term in terms(2 * (block + e)):
-                table += [DP[s] * term, gap]
-            for term in terms(2 * (block + e) + 1):
-                table += [DP[s, 4 : 4 + depth, :] * term]
+        for term in terms(2 * block):
+            table += [DP[s] * term, gap]
+        for term in terms(2 * block + 1):
+            table += [DP[s, 4 : 4 + depth, :] * term]
         table = jnp.concatenate(table, axis=0).astype(BF16)
         for c in range(4):
-            both = jnp.dot(
-                table, W[s, :, 256 * c : 256 * (c + 1)], preferred_element_type=F32
-            )
-            for e in range(2):
-                got = both[span * e : span * (e + 1)]
-                a = got[0:wide] + got[pad : pad + wide]
-                b = got[top : top + depth] + got[top + depth : top + 2 * depth]
-                for h in range(2):
-                    IA[s, block + e, 2 * c + h] = a[:, 128 * h : 128 * (h + 1)]
-                    IB[s, block + e, 2 * c + h] = b[:, 128 * h : 128 * (h + 1)]
+            got = jnp.dot(table, W[s, :, 256 * c : 256 * (c + 1)], preferred_element_type=F32)
+            a = got[0:wide] + got[pad : pad + wide]
+            b = got[top : top + depth] + got[top + depth : top + 2 * depth]
+            for h in range(2):
+                IA[parity][s, 2 * c + h] = a[:, 128 * h : 128 * (h + 1)]
+                IB[parity][s, 2 * c + h] = b[:, 128 * h : 128 * (h + 1)]
 
     def coefficients(m):
         at = rows(m)
@@ -387,14 +383,14 @@
     def first_step(slot, b, s, field, g, pulse, stored):
         p, m = 2 * s + field, 8 * g
         X, z = neighbours(N, (slot, p), m + 4, stored)
-        injected = IA[s, b, :, rows(m), :] if field else None
+        injected = IA[b][s, :, rows(m), :] if field else None
         new = advance(field, s, z(0), spread(X, z), M[p, OWN, rows(m), :], m, injected, pulse)
         put_field(M, (p,), m, new)
 
     def second_step(slot, to, b, s, field, g, pulse, final=False):
         p, m = 2 * s + field, 8 * g + 4
         X, z = neighbours(M, (p,), m, True)
-        injected = IB[s, b, :, rows(8 * g), :] if field else None
+        injected = IB[b][s, :, rows(8 * g), :] if field else None
         hi = N[slot, p, OWN, rows(8 * g + 8), :]
         centre = z(0)
         new = advance(field, s, centre, spread(X, z), hi, m, injected, pulse)
@@ -481,13 +477,14 @@
                 first_step(0, 0, s, field, g, pulse_of(s, 0), False)
             for g in (0, groups - 1):
                 second_step(0, 1, 0, s, field, g, pulse_of(s, 1))
+        for s in range(shots):
             each_way(send_now(1, 2 * s + field))
 
     first_edges(0)
     field_in(1)
     tables()
     for s in range(shots):
-        inject(s, 0)
+        inject(s, 0, 0)
     first_edges(1)
     for s in range(shots):
         for field in range(2):
@@ -498,20 +495,19 @@
         p = 2 * s + field
         each_way(arrive_now(slot, p))
         for g in (0, groups):
-            first_step(slot, b, s, field, g, pulses[0], False)
+            first_step(slot, slot, s, field, g, pulses[0], False)
         for g in (0, groups - 1):
-            second_step(slot, to, b, s, field, g, pulses[1])
+            second_step(slot, to, slot, s, field, g, pulses[1])
         each_way(send_now(to, p))
 
-    def inner(b, slot, to, s, pulses, products=False):
+    def inner(b, slot, to, s, pulses):
+        inject(s, to, b + 1)
         for field in range(2):
             for g in range(1, groups - 1):
-                second_step(slot, to, b, s, field, g, pulses[1])
-        if products:
-            inject(s, b + 1)
+                second_step(slot, to, slot, s, field, g, pulses[1])
         for field in range(2):
             for g in range(1, groups):
-                first_step(to, b + 1, s, field, g, pulses[2], True)
+                first_step(to, to, s, field, g, pulses[2], True)
 
     def pulses_of(s, b):
         return [pulse_of(s, 2 * b + j) for j in range(3)]
@@ -526,7 +522,7 @@
                 pulses = pulses_of(s, b)
                 for field in range(2):
                     edges(b, slot, to, s, field, pulses)
-                inner(b, slot, to, s, pulses, e == 0)
+                inner(b, slot, to, s, pulses)
         return carry
 
     lax.fori_loop(0, blocks // 2 - 1, two_blocks, 0)
@@ -565,7 +561,7 @@
         for s in range(shots):
             for field in range(2):
                 for g in wanted:
-                    second_step(slot, to, last, s, field, g, pulse_of(s, steps - 1), True)
+                    second_step(slot, to, slot, s, field, g, pulse_of(s, steps - 1), True)
 
     final_step(range(1, groups - 1))
     pair.wait()
@@ -592,7 +588,7 @@
         for field in range(2):
             each_way(arrive_now(slot, 2 * s + field))
             for g in (0, groups):
-                first_step(slot, last, s, field, g, pulse_of(s, 2 * last), False)
+                first_step(slot, slot, s, field, g, pulse_of(s, 2 * last), False)
 
     late = zeros
     for s in range(shots):
@@ -771,8 +767,8 @@
             pltpu.VMEM((planes, 16, wide, 128), F32),
             *[pltpu.VMEM((8, wide, 128), F32) for _ in range(6)],
             pltpu.VMEM((shots, 8, wide, 128), F32),
-            pltpu.VMEM((shots, steps // 2, 8, wide, 128), F32),
-            pltpu.VMEM((shots, steps // 2, 8, depth, 128), F32),
+            *[pltpu.VMEM((shots, 8, wide, 128), F32) for _ in range(2)],
+            *[pltpu.VMEM((shots, 8, depth, 128), F32) for _ in range(2)],
             pltpu.VMEM((shots, nrec, lateral), BF16),
             pltpu.VMEM((shots, wide, nrec), F32),
             pltpu.VMEM((2, lateral, 128), F32),

time: 94.1 us -> 92.8 us (0.986)
  Pallas kernels: 93.1 us -> 91.8 us
    pallas_call x1, Pallas kernels: 92 us -> 90.7 us  [local(): pl.pallas_call(functools.partial(kernel, steps), name='rtm_window', out_s...]
where the time goes in v4:
time: 92.8 us; the launch traced here: 92.7 us
  Pallas kernels  91.8 us (99%)
    pallas_call x1, Pallas kernels, local(): pl.pallas_call(functools.partial(kernel, steps), name='rtm_window', out_s...  90.7 us

profile of v4, /device:TPU:65, one launch (start us, length us, event | category | flops | bytes accessed | tf_op | source)
XLA Modules:
  0.0 92.7 jit_solution(12567290023331639706)
XLA Ops:
  0.6 90.7 %rtm_window.1 = (f32[8,64,128]{2,1,0:T(8,128)S(1)}, f32[2,64,1024]{2,1,0:T(8,128)S(1)}, f32[2,64,1024]{2,1,0:T(8,128)S(1)}) custom-call(f32[64,1024]{1,0:T(8,128)} %refs_0_.1, s32[64,1024]{1,0:T(8,128)} %refs_1_.1, f32[2,64,1024]{2,1,0:T(8,128)} %refs_2_.1, f32[2,64,1024]{2,1,0:T(8,128)} %refs_3_.1, f32[2,64,1024]{2,1,0:T(8,128)} %refs_4_.1, ...), custom_call_target="tpu_custom_call" | custom-call | tf_op jit(solution)/shard_map/rtm_window/pallas_call | solution.py:741
  91.4 1.1 %finish.1 = (f32[64,1024]{1,0:T(8,128)}, f32[2,64,1024]{2,1,0:T(8,128)}, f32[2,64,1024]{2,1,0:T(8,128)}) custom-call(f32[8,64,128]{2,1,0:T(8,128)S(1)} %get-tuple-element.6.image, f32[2,64,1024]{2,1,0:T(8,128)S(1)} %get-tuple-element.7.src, f32[2,64,1024]{2,1,0:T(8,128)S(1)} %get-tuple-element.8.rec), custom_call_target="tpu_custom_call" | custom-call | tf_op jit(solution)/shard_map/finish/pallas_call | solution.py:824
